TPU v7x, 8 devices: a whole 2x2x1 slice. The times are simulated.
8 devices in a mesh: dp: 1 (over z), cp: 2 (over y), tp: 4 (over x, core).
Axes of the slice: x: 2, y: 2, z: 1, core: 2. Of those that a mesh axis runs over, the one named last changes fastest.
Arguments:
- x_tok: bfloat16 [3072, 1536], P(('dp', 'cp', 'tp'))
- w_q: bfloat16 [1536, 48, 32], P(None, 'tp')
- w_k: bfloat16 [1536, 8, 32], P(None, 'tp')
- w_v: bfloat16 [1536, 8, 32], P(None, 'tp')
- w_o: bfloat16 [48, 32, 1536], P('tp')
- expert_ids: int32 [3072, 2], P(('dp', 'cp', 'tp'))
- gate_wts: float32 [3072, 2], P(('dp', 'cp', 'tp'))
- w_gate: bfloat16 [16, 1536, 2048], P(('cp', 'tp'))
- w_up: bfloat16 [16, 1536, 2048], P(('cp', 'tp'))
- w_down: bfloat16 [16, 2048, 1536], P(('cp', 'tp'))
Outputs:
- output: bfloat16 [3072, 1536], P(('dp', 'cp', 'tp'))
All inputs are finite; a program needn't handle non-finite values.
Results may differ from a plain program's by a relative error of at most 0.0104868.
Values are sent between devices in bfloat16 or wider.
A program may use at most 1 GiB of HBM per device.

v0:
```python
import jax
import jax.numpy as jnp
from jax import lax
from jax.sharding import PartitionSpec as P


def seq_positions(cp_index, n_cp, half_len):
    chunk_len = half_len // 2
    in_half = jnp.arange(half_len)
    return jnp.where(in_half < chunk_len, cp_index * chunk_len + in_half, (2 * n_cp - 1 - cp_index) * chunk_len + in_half - chunk_len)


def attend_block(q_loc, k_blk, v_blk, q_pos, k_pos, run_max, run_sum, run_acc):
    head_dim = q_loc.shape[-1]
    scores = jnp.einsum("qgrd,kgd->grqk", q_loc, k_blk, preferred_element_type=jnp.float32) * (head_dim ** -0.5)
    allowed = q_pos[:, None] >= k_pos[None, :]
    scores = jnp.where(allowed, scores, -1e30)
    new_max = jnp.maximum(run_max, jnp.max(scores, axis=-1))
    prob_vals = jnp.exp(scores - new_max[..., None])
    rescale = jnp.exp(run_max - new_max)
    new_sum = run_sum * rescale + jnp.sum(prob_vals, axis=-1)
    new_acc = run_acc * rescale[..., None] + jnp.einsum("grqk,kgd->grqd", prob_vals.astype(jnp.bfloat16), v_blk, preferred_element_type=jnp.float32)
    return new_max, new_sum, new_acc


def solution(mesh):
    n_cp = mesh.shape["cp"]
    n_tp = mesh.shape["tp"]
    row_spec = P(("dp", "cp", "tp"), None)
    head_spec = P(None, "tp", None)
    expert_spec = P(("cp", "tp"), None, None)

    def device_step(x_loc, w_q, w_k, w_v, w_o, ids_loc, gates_loc, w_gate, w_up, w_down):
        tok_dev, hid_dim = x_loc.shape
        top_k = ids_loc.shape[1]
        kv_loc = w_k.shape[1]
        head_dim = w_q.shape[2]
        grp_size = w_q.shape[1] // kv_loc
        local_exp = w_gate.shape[0]
        n_experts = local_exp * n_cp * n_tp // 2
        capacity = top_k * tok_dev // n_experts
        half_hid = hid_dim // 2
        cp_index = lax.axis_index("cp")
        tp_index = lax.axis_index("tp")

        x_half = lax.all_gather(x_loc, "tp", axis=0, tiled=True)
        half_len = x_half.shape[0]
        q_loc = jnp.einsum("sh,hnd->snd", x_half, w_q, preferred_element_type=jnp.float32).astype(jnp.bfloat16).reshape(half_len, kv_loc, grp_size, head_dim)
        k_cur = jnp.einsum("sh,hnd->snd", x_half, w_k, preferred_element_type=jnp.float32).astype(jnp.bfloat16)
        v_cur = jnp.einsum("sh,hnd->snd", x_half, w_v, preferred_element_type=jnp.float32).astype(jnp.bfloat16)
        q_pos = seq_positions(cp_index, n_cp, half_len)
        init_max = jnp.full((kv_loc, grp_size, half_len), -1e30, jnp.float32)
        init_sum = jnp.zeros((kv_loc, grp_size, half_len), jnp.float32)
        init_acc = jnp.zeros((kv_loc, grp_size, half_len, head_dim), jnp.float32)
        first_state = attend_block(q_loc, k_cur, v_cur, q_pos, q_pos, init_max, init_sum, init_acc)
        shift_perm = [(src_dev, (src_dev + 1) % n_cp) for src_dev in range(n_cp)]

        def kv_step(step_idx, kv_state):
            k_blk, v_blk, cur_max, cur_sum, cur_acc = kv_state
            k_blk = lax.ppermute(k_blk, "cp", shift_perm)
            v_blk = lax.ppermute(v_blk, "cp", shift_perm)
            k_pos = seq_positions((cp_index - step_idx) % n_cp, n_cp, half_len)
            cur_max, cur_sum, cur_acc = attend_block(q_loc, k_blk, v_blk, q_pos, k_pos, cur_max, cur_sum, cur_acc)
            return k_blk, v_blk, cur_max, cur_sum, cur_acc

        kv_state = lax.fori_loop(1, n_cp, kv_step, (k_cur, v_cur) + first_state)
        attn_out = (kv_state[4] / kv_state[3][..., None]).astype(jnp.bfloat16)
        w_o_view = w_o.reshape(kv_loc, grp_size, head_dim, hid_dim)
        attn_part = jnp.einsum("grqd,grdh->qh", attn_out, w_o_view, preferred_element_type=jnp.float32)
        attn_rows = lax.psum_scatter(attn_part, "tp", scatter_dimension=0, tiled=True)
        h_loc = (x_loc.astype(jnp.float32) + attn_rows).astype(jnp.bfloat16)

        flat_ids = ids_loc.reshape(-1)
        one_hot = (flat_ids[:, None] == jnp.arange(n_experts)[None, :]).astype(jnp.int32)
        slot_ids = jnp.sum(jnp.cumsum(one_hot, axis=0) * one_hot, axis=1) - 1
        dest_idx = flat_ids * capacity + slot_ids
        choice_rows = jnp.arange(tok_dev * top_k, dtype=jnp.int32) // top_k
        slot_rows = jax.ops.segment_sum(choice_rows, dest_idx, num_segments=n_experts * capacity)
        send_buf = jnp.take(h_loc, slot_rows, axis=0).reshape(n_cp, n_tp // 2, 1, local_exp, capacity, hid_dim)
        send_buf = jnp.broadcast_to(send_buf, (n_cp, n_tp // 2, 2, local_exp, capacity, hid_dim)).reshape(n_cp, n_tp, local_exp, capacity, hid_dim)
        recv_buf = lax.all_to_all(send_buf, "tp", 1, 1, tiled=True)
        recv_buf = lax.all_to_all(recv_buf, "cp", 0, 0, tiled=True)

        gate_pre = jnp.einsum("uvech,ehf->uvecf", recv_buf, w_gate, preferred_element_type=jnp.float32)
        up_pre = jnp.einsum("uvech,ehf->uvecf", recv_buf, w_up, preferred_element_type=jnp.float32)
        hidden = (jax.nn.silu(gate_pre) * up_pre).astype(jnp.bfloat16)
        z_part = jnp.einsum("uvecf,efh->uvech", hidden, w_down, preferred_element_type=jnp.float32)

        my_half = tp_index % 2
        keep_part = lax.dynamic_slice_in_dim(z_part, my_half * half_hid, half_hid, axis=4)
        send_part = lax.dynamic_slice_in_dim(z_part, (1 - my_half) * half_hid, half_hid, axis=4)
        pair_perm = [(dev_idx, dev_idx ^ 1) for dev_idx in range(n_tp)]
        z_half = (keep_part + lax.ppermute(send_part, "tp", pair_perm)).astype(jnp.bfloat16)

        back_buf = lax.all_to_all(z_half, "cp", 0, 0, tiled=True)
        back_buf = lax.all_to_all(back_buf, "tp", 1, 1, tiled=True)
        z_full = back_buf.reshape(n_cp, n_tp // 2, 2, local_exp, capacity, half_hid).transpose(0, 1, 3, 4, 2, 5).reshape(n_experts * capacity, hid_dim)
        picked = jnp.take(z_full, dest_idx, axis=0).reshape(tok_dev, top_k, hid_dim)
        y_loc = h_loc.astype(jnp.float32) + jnp.sum(gates_loc[:, :, None] * picked, axis=1)
        return y_loc.astype(jnp.bfloat16)

    return jax.shard_map(device_step, mesh=mesh, in_specs=(row_spec, head_spec, head_spec, head_spec, P("tp", None, None), row_spec, row_spec, expert_spec, expert_spec, expert_spec), out_specs=row_spec, check_vma=False)
```

profile of v0, /device:TPU:0, one launch (start us, length us, event | category | flops | bytes accessed | tf_op | source)
XLA Modules:
  0.0 688.7 jit_solution(11303618931638743369)
XLA Ops:
  7.4 3.5 broadcast_compare_fusion
  10.9 35.4 %all-gather.2.cloned.1.call-done = bf16[1536,1536]{1,0:T(8,128)(2,1)} async-done(((bf16[384,1536]{1,0:T(8,128)(2,1)}), bf16[1536,1536]{1,0:T(8,128)(2,1)}) %all-gather.2.cloned.1.call-update) | async-done | bytes 4718608 | tf_op jit(solution)/shard_map/all_gather | solution.py:46
  46.3 4.7 bitcast_convert_fusion
  52.4 2.0 fusion.60
  58.4 42.4 %fusion.4 = (f32[2,6,1536]{2,1,0:T(8,128)}, f32[2,1536,1536,6]{2,1,3,0:T(8,128)}) fusion(pred[1536,1536]{0,1:T(8,128)(4,1)} %get-tuple-element.42, bf16[1536,2,6,32]{0,3,2,1:T(8,128)(2,1)} %bitcast.139, bf16[1536,2,32]{0,2,1:T(8,128)(2,1)} %bitcast_convert_fusion), kind=kOutput, calls=%fused_computation.11 | convolution fusion | flops 1896855552 | bytes 117055488 | tf_op jit(solution)/shard_map/qgrd,kgd->grqk/dot_general | solution.py:15
  100.8 42.3 %fusion.5 = (f32[2,6,1536]{2,1,0:T(8,128)}, f32[2,1536,1536,6]{2,1,3,0:T(8,128)}) fusion(pred[1536,1536]{0,1:T(8,128)(4,1)S(1)} %get-tuple-element.40, bf16[1536,2,6,32]{0,3,2,1:T(8,128)(2,1)} %bitcast.140, bf16[1536,2,32]{0,2,1:T(8,128)(2,1)} %collective-permute-done), kind=kOutput, calls=%fused_computation.12 | convolution fusion | flops 1896855552 | bytes 117055488 | tf_op jit(solution)/shard_map/while/body/eval_jaxpr/qgrd,kgd->grqk/dot_general | solution.py:15
  144.1 71.8 %fusion = (f32[2,6,1536]{2,1,0:T(8,128)S(1)}, f32[2,6,1536]{2,1,0:T(8,128)S(1)}) fusion(f32[2,1536,1536,6]{2,1,3,0:T(8,128)} %get-tuple-element.45, f32[2,6,1536]{2,1,0:T(8,128)S(1)} %get-tuple-element.29, pred[1536,1536]{0,1:T(8,128)(4,1)} %get-tuple-element.42, f32[2,6,1536]{2,1,0:T(8,128)S(1)} %get-tuple-element.28, ...), kind=kLoop, calls=%fused_computation.7 | loop fusion | flops 226455552 | bytes 231505920 | tf_op jit(solution)/shard_map/reduce_sum | solution.py:21
  216.0 40.1 %fusion.30 = f32[2,6,1536,32]{2,3,1,0:T(8,128)} fusion(f32[2,1536,1536,6]{2,1,3,0:T(8,128)} %get-tuple-element.45, f32[2,6,1536]{2,1,0:T(8,128)S(1)} %get-tuple-element.29, pred[1536,1536]{0,1:T(8,128)(4,1)} %get-tuple-element.42, f32[2,6,1536]{2,1,0:T(8,128)S(1)} %get-tuple-element.26, f32[2,6,1536]{2,1,0:T(8,128)S(1)} %get-tuple-element.27, ...), kind=kOutput, calls=%fused_computation.42 | convolution fusion | flops 1926365184 | bytes 118382592 | tf_op jit(solution)/shard_map/grqk,kgd->grqd/dot_general | solution.py:22
  256.1 39.9 %divide_convert_fusion = bf16[2,6,1536,32]{2,3,1,0:T(8,128)(2,1)} fusion(f32[2,6,1536,32]{2,3,1,0:T(8,128)} %fusion.30, f32[2,1536,1536,6]{2,1,3,0:T(8,128)} %get-tuple-element.47, f32[2,6,1536]{2,1,0:T(8,128)S(1)} %get-tuple-element.28, pred[1536,1536]{0,1:T(8,128)(4,1)S(1)} %get-tuple-element.40, f32[2,6,1536]{2,1,0:T(8,128)S(1)} %get-tuple-element.25, ...), kind=kOutput, calls=%fused_computation.46 | convolution fusion | flops 1926955008 | bytes 119488512 | tf_op jit(solution)/shard_map/while/body/eval_jaxpr/grqk,kgd->grqd/dot_general | solution.py:22
  296.0 6.4 convolution_bitcast_fusion
  306.2 5.9 scatter_custom_fusion
  312.7 61.5 %reduce-scatter.2.cloned.1.call-done = f32[384,1536]{1,0:T(8,128)} async-done(((f32[1536,1536]{1,0:T(8,128)}), f32[384,1536]{1,0:T(8,128)}) %reduce-scatter.2.cloned.1.call-update) | async-done | bytes 2359312 | tf_op jit(solution)/shard_map/reduce_scatter | solution.py:70
  374.2 2.0 add_convert_fusion.1
  376.2 3.8 gather_fusion
  380.0 1.9 broadcast_select_fusion.1
  382.7 56.3 %all_to_all.20 = bf16[2,4,2,96,1536]{4,3,0,2,1:T(8,128)(2,1)S(1)} all-to-all(bf16[2,4,2,96,1536]{4,3,0,2,1:T(8,128)(2,1)S(1)} %bitcast.134), channel_id=1, replica_groups=mesh['dp'=1,'cp'=2,'tp'=4] {'tp'}, dimensions={1} | all-to-all | bytes 9437184 | tf_op jit(solution)/shard_map/all_to_all | solution.py:81
  439.1 2.4 copy.51
  441.5 5.8 all-to-all-start.1
  447.4 52.6 %all-to-all-done.1 = bf16[2,4,2,96,1536]{4,3,1,2,0:T(8,128)(2,1)} async-done(((bf16[2,4,2,96,1536]{4,3,1,2,0:T(8,128)(2,1)}), bf16[2,4,2,96,1536]{4,3,1,2,0:T(8,128)(2,1)}, u32[]{:S(2)}, u32[]{:S(2)}) %all-to-all-start.1) | async-done | bytes 4718624 | tf_op jit(solution)/shard_map/all_to_all | solution.py:82
  499.9 17.2 %fusion.14 = f32[2,2,4,96,2048]{4,3,2,1,0:T(8,128)} fusion(bf16[2,1536,2048]{2,1,0:T(8,128)(2,1)} %param.18, bf16[2,4,2,96,1536]{4,3,1,2,0:T(8,128)(2,1)} %all-to-all-done.1), kind=kOutput, calls=%fused_computation.19 | convolution fusion | flops 9663676416 | bytes 29884416 | tf_op jit(solution)/shard_map/uvech,ehf->uvecf/dot_general | solution.py:85
  517.2 16.9 %fusion.16 = f32[2,2,4,96,2048]{4,3,2,1,0:T(8,128)} fusion(bf16[2,1536,2048]{2,1,0:T(8,128)(2,1)} %param.17, bf16[2,4,2,96,1536]{4,3,1,2,0:T(8,128)(2,1)} %all-to-all-done.1), kind=kOutput, calls=%fused_computation.21 | convolution fusion | flops 9663676416 | bytes 29884416 | tf_op jit(solution)/shard_map/uvech,ehf->uvecf/dot_general | solution.py:84
  534.0 20.4 %fusion.12 = f32[2,2,4,96,1536]{4,3,2,1,0:T(8,128)} fusion(bf16[2,2048,1536]{2,1,0:T(8,128)(2,1)} %param.19, f32[2,2,4,96,2048]{4,3,2,1,0:T(8,128)} %fusion.14, f32[2,2,4,96,2048]{4,3,2,1,0:T(8,128)} %fusion.16), kind=kOutput, calls=%fused_computation.17 | convolution fusion | flops 9682550784 | bytes 47185920 | tf_op jit(solution)/shard_map/uvecf,efh->uvech/dot_general | solution.py:87
  554.5 4.9 dynamic-slice_bitcast_fusion
  559.4 7.9 %collective-permute-done.2 = f32[2,4,2,96,768]{4,3,1,0,2:T(8,128)} collective-permute-done((f32[2,4,2,96,768]{4,3,1,0,2:T(8,128)}, f32[2,4,2,96,768]{4,3,1,0,2:T(8,128)}, u32[]{:S(2)}, u32[]{:S(2)}) %collective-permute-start.2) | collective-permute-done | bytes 4718624 | tf_op jit(solution)/shard_map/ppermute | solution.py:93
  567.3 4.3 fusion.24
  571.8 30.8 %all_to_all.21 = bf16[2,4,2,96,768]{4,3,1,2,0:T(8,128)(2,1)S(1)} all-to-all(bf16[2,4,2,96,768]{4,3,1,2,0:T(8,128)(2,1)S(1)} %copy.54), channel_id=1, replica_groups=mesh['dp'=1,'cp'=2,'tp'=4] {'cp'}, dimensions={0} | all-to-all | bytes 4718592 | tf_op jit(solution)/shard_map/all_to_all | solution.py:95
  604.2 4.7 all-to-all-start.3
  609.6 27.6 %all-to-all-done.3 = bf16[2,4,2,96,768]{4,3,0,2,1:T(8,128)(2,1)} async-done(((bf16[2,4,2,96,768]{4,3,0,2,1:T(8,128)(2,1)}), bf16[2,4,2,96,768]{4,3,0,2,1:T(8,128)(2,1)}, u32[]{:S(2)}, u32[]{:S(2)}) %all-to-all-start.3) | async-done | bytes 2359328 | tf_op jit(solution)/shard_map/all_to_all | solution.py:96
  637.1 4.1 copy.56
  643.0 7.9 %gather_fusion.1 = bf16[768,1536]{1,0:T(8,128)(2,1)} fusion(bf16[768,1536]{1,0:T(8,128)(2,1)} %bitcast.133, s32[1024]{0:T(1024)S(1)} %pad_clamp_fusion), kind=kCustom, calls=%fused_computation.1 | custom fusion | bytes 4721664 | tf_op jit(solution)/shard_map/jit(_take)/gather | solution.py:98
  650.9 5.8 gather.15
  656.7 23.3 %multiply_reduce_fusion = f32[384,1536]{1,0:T(8,128)S(1)} fusion(bf16[384,2,1536]{2,1,0:T(2,128)(2,1)} %gather.15, pred[384,2]{1,0:T(8,128)(4,1)S(1)} %copy.48, f32[384,2]{1,0:T(8,128)S(1)} %copy.42), kind=kLoop, calls=%fused_computation.34 | loop fusion | flops 4128768 | bytes 4722432 | tf_op jit(solution)/shard_map/reduce_sum | solution.py:99
  (68 shorter events, 17.9 us)
Async XLA Ops:
  6.5 289.5 %copy-start = (bf16[12,32,1536]{2,1,0:T(8,128)(2,1)S(1)}, bf16[12,32,1536]{2,1,0:T(8,128)(2,1)}, u32[]{:S(2)}) copy-start(bf16[12,32,1536]{2,1,0:T(8,128)(2,1)} %param.14) | copy-start | bytes 3538948
  6.5 39.7 %all-gather.2.cloned.1.call-start = ((), (), s32[]{:S(2)}) async-start(), calls=%async_computation.5 | async-start | bytes 5898240 | tf_op jit(solution)/shard_map/all_gather | solution.py:46
  7.3 366.9 %reduce-scatter.2.cloned.1.call-start = ((), (), s32[]{:S(2)}) async-start(), calls=%async_computation.6 | async-start | bytes 11796480 | tf_op jit(solution)/shard_map/reduce_scatter | solution.py:70
  46.3 6.2 copy-start.1
  46.3 6.2 copy-start.9
  51.0 49.9 %collective-permute-start = (bf16[1536,2,32]{0,2,1:T(8,128)(2,1)}, bf16[1536,2,32]{0,2,1:T(8,128)(2,1)}, u32[]{:S(2)}, u32[]{:S(2)}) collective-permute-start(bf16[1536,2,32]{0,2,1:T(8,128)(2,1)} %bitcast_convert_fusion), channel_id=1, source_target_pairs={{0,4},{4,0},{1,5},{5,1},{2,6},{6,2},{3,7},{7,3}} | collective-permute-start | bytes 589832 | tf_op jit(solution)/shard_map/while/body/eval_jaxpr/ppermute | solution.py:60
  52.4 3.2 copy-start.5
  57.8 198.2 %collective-permute-start.1 = (bf16[1536,2,32]{0,2,1:T(8,128)(2,1)}, bf16[1536,2,32]{0,2,1:T(8,128)(2,1)}, u32[]{:S(2)}, u32[]{:S(2)}) collective-permute-start(bf16[1536,2,32]{0,2,1:T(8,128)(2,1)} %convert_element_type.49), channel_id=1, source_target_pairs={{0,4},{4,0},{1,5},{5,1},{2,6},{6,2},{3,7},{7,3}} | collective-permute-start | bytes 589832 | tf_op jit(solution)/shard_map/while/body/eval_jaxpr/ppermute | solution.py:61
  144.1 71.8 %copy-start.3 = (f32[2,6,1536]{2,1,0:T(8,128)S(1)}, f32[2,6,1536]{2,1,0:T(8,128)}, u32[]{:S(2)}) copy-start(f32[2,6,1536]{2,1,0:T(8,128)} %get-tuple-element.44) | copy-start | bytes 221188
  144.1 71.8 %copy-start.4 = (f32[2,6,1536]{2,1,0:T(8,128)S(1)}, f32[2,6,1536]{2,1,0:T(8,128)}, u32[]{:S(2)}) copy-start(f32[2,6,1536]{2,1,0:T(8,128)} %get-tuple-element.46) | copy-start | bytes 221188
  302.4 0.7 copy-start.6
  302.4 71.8 %copy-start.2 = (bf16[384,1536]{1,0:T(8,128)(2,1)S(1)}, bf16[384,1536]{1,0:T(8,128)(2,1)}, u32[]{:S(2)}) copy-start(bf16[384,1536]{1,0:T(8,128)(2,1)} %param.10) | copy-start | bytes 3538948
  376.2 3.8 copy-start.7
  441.5 58.4 %all-to-all-start.1 = ((bf16[2,4,2,96,1536]{4,3,1,2,0:T(8,128)(2,1)}), bf16[2,4,2,96,1536]{4,3,1,2,0:T(8,128)(2,1)}, u32[]{:S(2)}, u32[]{:S(2)}) async-start(bf16[2,4,2,96,1536]{4,3,1,2,0:T(8,128)(2,1)} %copy.51), calls=%async_computation.2 | async-start | bytes 9437184 | tf_op jit(solution)/shard_map/all_to_all | solution.py:82
  559.4 7.9 %collective-permute-start.2 = (f32[2,4,2,96,768]{4,3,1,0,2:T(8,128)}, f32[2,4,2,96,768]{4,3,1,0,2:T(8,128)}, u32[]{:S(2)}, u32[]{:S(2)}) collective-permute-start(f32[2,4,2,96,768]{4,3,1,0,2:T(8,128)} %dynamic-slice_bitcast_fusion), channel_id=1, source_target_pairs={{0,1},{1,0},{2,3},{3,2},{4,5},{5,4},{6,7},{7,6}} | collective-permute-start | bytes 14155784 | tf_op jit(solution)/shard_map/ppermute | solution.py:93
  602.6 6.8 copy-start.8
  604.2 33.0 %all-to-all-start.3 = ((bf16[2,4,2,96,768]{4,3,0,2,1:T(8,128)(2,1)}), bf16[2,4,2,96,768]{4,3,0,2,1:T(8,128)(2,1)}, u32[]{:S(2)}, u32[]{:S(2)}) async-start(bf16[2,4,2,96,768]{4,3,0,2,1:T(8,128)(2,1)} %copy.55), calls=%async_computation.4 | async-start | bytes 4718592 | tf_op jit(solution)/shard_map/all_to_all | solution.py:96
Sparse Core Ops, SparseCore 0:
  8.9 37.3 all-gather.1
  302.6 71.5 reduce-scatter.1
where the time goes:
time: 696 us; the launch traced here: 689 us
  matrix products  234 us (34%)
  waiting for transfers between devices  186 us (27%)
  other arithmetic  119 us (17%)
  blocking collectives  87.2 us (13%)
  local copies, waits for them, and re-layouts  36.2 us (5%)
  between operations  14.2 us (2%)
  starting transfers between devices  12.6 us (2%)
    dot_general x2, matrix products, attend_block(): jnp.einsum('qgrd,kgd->grqk', q_loc, k_blk, preferred_element_type=jnp.flo...  84.7 us
    dot_general x2, matrix products, attend_block(): jnp.einsum('grqk,kgd->grqd', prob_vals.astype(jnp.bfloat16), v_blk, prefe...  80 us
    reduce_sum x1, other arithmetic, attend_block(): new_sum = run_sum * rescale + jnp.sum(prob_vals, axis=-1)  71.8 us
    reduce_scatter x1, waiting for transfers between devices, device_step(): lax.psum_scatter(attn_part, 'tp', scatter_dimension=0, tiled=True)  61.5 us
    all_to_all x1, blocking collectives, device_step(): recv_buf = lax.all_to_all(send_buf, 'tp', 1, 1, tiled=True)  56.3 us
    all_to_all x1, waiting for transfers between devices, device_step(): recv_buf = lax.all_to_all(recv_buf, 'cp', 0, 0, tiled=True)  52.6 us
    all_gather x1, waiting for transfers between devices, device_step(): x_half = lax.all_gather(x_loc, 'tp', axis=0, tiled=True)  35.4 us
    all_to_all x1, blocking collectives, device_step(): back_buf = lax.all_to_all(z_half, 'cp', 0, 0, tiled=True)  30.8 us
  transfers between devices with their start and end apart: 7, of which 5 were waited for; matrix products, arithmetic and copies ran while one was open for 31% of the time, Pallas kernels for 0%

commit v1 on v0

v1 whole, which is shorter than its diff:
```python
import functools
import math

import jax
import jax.numpy as jnp
from jax import lax
from jax.experimental import pallas as pl
from jax.experimental.pallas import tpu as pltpu
from jax.sharding import PartitionSpec as P

MESH = pl.DeviceIdType.MESH
F32 = jnp.float32
BF16 = jnp.bfloat16

NT = (((1,), (1,)), ((), ()))
QT = 128
KC = 256


def dot(a, b):
    return jnp.dot(a, b, preferred_element_type=F32)


def dot_nt(a, b):
    return lax.dot_general(a, b, NT, preferred_element_type=F32)


def remote(src, dst, send, recv, **dev):
    return pltpu.make_async_remote_copy(src_ref=src, dst_ref=dst, send_sem=send, recv_sem=recv, device_id=dev, device_id_type=MESH)


def attn_kernel(x, wq_h, wk_h, wv_h, wo_h, wg, wu, wd,
                h_out, wg_r, wu_r, wd_r,
                xh, wq, wkv, wo, kvown, kvrecv, kaug, vt, qaug, osend, orecv, m_s, l_s, acc_s,
                loc_sem, xf_s, xf_r, xp_s, xp_r, xw_s, xw_r, kv_s, kv_r, wo_s, wo_r, ew_s, ew_r, o_s, o_r):
    c = lax.axis_index("cp")
    t = lax.axis_index("tp")
    s = lax.rem(t, 2)
    part = t + 1 - 2 * s
    far = lax.rem(t + 2, 4)
    farp = lax.rem(part + 2, 4)
    cn = 1 - c
    tok = xh.shape[1]
    nr = tok // QT
    chunk = 2 * tok
    hid = x.shape[1]
    heads = wq_h.shape[0] // 32
    npair = heads // 2
    scale = 32 ** -0.5 * math.log2(math.e)

    bar = pltpu.get_barrier_semaphore()
    pl.semaphore_signal(bar, inc=1, device_id={"tp": part}, device_id_type=MESH)
    pl.semaphore_signal(bar, inc=1, device_id={"tp": far}, device_id_type=MESH)
    pl.semaphore_signal(bar, inc=1, device_id={"tp": farp}, device_id_type=MESH)
    pl.semaphore_signal(bar, inc=1, device_id={"cp": cn}, device_id_type=MESH)

    locs = [
        pltpu.make_async_copy(x, xh.at[t], loc_sem.at[0]),
        pltpu.make_async_copy(wq_h, wq, loc_sem.at[1]),
        pltpu.make_async_copy(wk_h, wkv.at[pl.ds(0, 64)], loc_sem.at[2]),
        pltpu.make_async_copy(wv_h, wkv.at[pl.ds(64, 64)], loc_sem.at[3]),
        pltpu.make_async_copy(wo_h, wo.at[t], loc_sem.at[4]),
    ]
    for cp_ in locs:
        cp_.start()
    pl.semaphore_wait(bar, 4)

    xfar = [remote(x.at[pl.ds(k * QT, QT)], xh.at[t, pl.ds(k * QT, QT)], xf_s.at[k], xf_r.at[k], tp=far) for k in range(nr)]
    xpart = remote(x, xh.at[t], xp_s, xp_r, tp=part)
    xfwd = [remote(xh.at[far, pl.ds(k * QT, QT)], xh.at[far, pl.ds(k * QT, QT)], xw_s.at[k], xw_r.at[k], tp=part) for k in range(nr)]
    for k in range(nr):
        xfar[k].start()
    xpart.start()

    qaug[:, :, 96:128, :] = jnp.zeros((qaug.shape[0], npair, 32, 2 * QT), BF16)

    def project(b):
        xb = xh[b]
        qt = dot_nt(wq[...], xb).astype(BF16)
        qs = qt.astype(F32) * scale
        h1 = qs.astype(BF16)
        r1 = qs - h1.astype(F32)
        h2 = r1.astype(BF16)
        h3 = (r1 - h2.astype(F32)).astype(BF16)
        for r in range(nr):
            for hd in range(heads):
                for k, part_v in enumerate((h1, h2, h3)):
                    qaug[b * nr + r, hd // 2, k * 32:(k + 1) * 32, (hd % 2) * QT:(hd % 2 + 1) * QT] = part_v[hd * 32:(hd + 1) * 32, r * QT:(r + 1) * QT]
        kvown[b] = dot_nt(wkv[...], xb).astype(BF16)

    def kvcopy(b):
        return remote(kvown.at[b], kvrecv.at[b], kv_s.at[b], kv_r.at[b], cp=cn)

    for cp_ in locs[:4]:
        cp_.wait()
    project(t)
    kvcopy(t).start()
    xpart.wait_recv()
    project(part)
    kvcopy(part).start()
    for k in range(nr):
        xfar[k].wait_recv()
        xfwd[k].start()
    project(far)
    kvcopy(far).start()
    for k in range(nr):
        xfwd[k].wait_recv()
    project(farp)
    kvcopy(farp).start()
    for k in range(nr):
        xfar[k].wait_send()
        xfwd[k].wait_send()
    xpart.wait_send()

    locs[4].wait()
    wofar = remote(wo_h, wo.at[t], wo_s.at[0], wo_r.at[0], tp=far)
    wopart = remote(wo_h, wo.at[t], wo_s.at[1], wo_r.at[1], tp=part)
    wofwd = remote(wo.at[far], wo.at[far], wo_s.at[2], wo_r.at[2], tp=part)
    wofar.start()
    wopart.start()

    zero_pad = jnp.zeros((32, tok), BF16)

    def place(b, src, cc):
        second = b // 2
        ck = cc * (1 - second) + (3 - cc) * second
        pos = pl.multiple_of(ck * chunk + lax.rem(b, 2) * tok, QT)
        kv = src[b]
        for g in range(2):
            kt = kv[g * 32:(g + 1) * 32]
            kaug[g, pl.ds(pos, tok), :] = jnp.concatenate([kt, kt, kt, zero_pad], axis=0).T
        vt[:, pl.ds(pos, tok)] = kv[64:128]

    def place_own(b, carry):
        place(b, kvown, c)
        return carry

    def place_recv(b, carry):
        kvcopy(b).wait_recv()
        place(b, kvrecv, cn)
        return carry

    lax.fori_loop(0, 4, place_own, 0)
    lax.fori_loop(0, 4, place_recv, 0)

    def ocopy(i, b, r):
        return remote(osend.at[i], orecv.at[pl.ds(r * QT, QT), pl.ds(t * tok, tok)], o_s.at[i], o_r.at[t, r], tp=b)

    def tile_of(ii):
        kk = ii // nr
        r = lax.rem(ii, nr)
        xb = lax.rem(t // 2 + 1 - kk // 2, 2)
        sb = lax.rem(s + lax.rem((kk + 1) // 2, 2), 2)
        return 2 * xb + sb, r

    def wcopy(ii):
        out = []
        for w, wr in ((wg, wg_r), (wu, wu_r)):
            n = w.shape[1] // (4 * nr)
            sl = pl.ds(pl.multiple_of(ii * n, n), n)
            k = 0 if w is wg else 1
            out.append(remote(w.at[1 - s, sl], wr.at[sl], ew_s.at[k], ew_r.at[k], tp=part))
        return out

    def wdcopy(ii):
        n = wd.shape[1] // 8
        sl = pl.ds(pl.multiple_of(ii * n, n), n)
        return remote(wd.at[1 - s, sl], wd_r.at[sl], ew_s.at[2], ew_r.at[2], tp=part)

    def tile(ii, carry):
        for cp_ in wcopy(ii):
            cp_.start()

        @pl.when(ii < 8)
        def _():
            wdcopy(ii).start()

        @pl.when(ii == 2 * nr)
        def _():
            wofar.wait_recv()
            wofwd.start()

        b, r = tile_of(ii)
        i = b * nr + r
        second = b // 2
        ck = c * (1 - second) + (3 - c) * second
        qpos = ck * chunk + lax.rem(b, 2) * tok + r * QT
        nfull = qpos // KC
        m_s[...] = jnp.full(m_s.shape, -jnp.inf, F32)
        l_s[...] = jnp.zeros(l_s.shape, F32)
        acc_s[...] = jnp.zeros(acc_s.shape, F32)

        def step(j, masked):
            k0 = pl.multiple_of(j * KC, KC)
            if masked:
                key_i = lax.broadcasted_iota(jnp.int32, (KC, 2 * QT), 0) + k0
                q_i = lax.rem(lax.broadcasted_iota(jnp.int32, (KC, 2 * QT), 1), QT) + qpos
                allowed = key_i <= q_i
            for p in range(npair):
                g = p // (npair // 2)
                sc = dot(kaug[g, pl.ds(k0, KC), :], qaug[i, p])
                if masked:
                    sc = jnp.where(allowed, sc, -jnp.inf)
                s8 = sc.reshape(KC // 8, 8, 2 * QT)
                mx = jnp.max(jnp.max(s8, axis=0), axis=0, keepdims=True)
                m_old = m_s[p]
                m_new = jnp.maximum(m_old, mx)
                alpha = jnp.exp2(m_old - m_new)
                pr = jnp.exp2(sc - m_new)
                l_s[p] = l_s[p] * alpha + jnp.sum(pr.reshape(KC // 8, 8, 2 * QT), axis=0)
                pv = dot(vt[g * 32:(g + 1) * 32, pl.ds(k0, KC)], pr.astype(BF16))
                acc_s[p] = acc_s[p] * alpha + pv
                m_s[p] = m_new

        def body(j, cc):
            step(j, False)
            return cc

        lax.fori_loop(0, nfull, body, 0)
        step(nfull, True)

        pieces = []
        for p in range(npair):
            o = acc_s[p] / jnp.sum(l_s[p], axis=0, keepdims=True)
            pieces += [o[:, :QT], o[:, QT:]]
        tile_o = jnp.concatenate(pieces, axis=0).T.astype(BF16)

        @pl.when(ii < 3 * nr)
        def _():
            osend[i] = tile_o
            ocopy(i, b, r).start()

        @pl.when(ii >= 3 * nr)
        def _():
            orecv[pl.ds(pl.multiple_of(r * QT, QT), QT), pl.ds(pl.multiple_of(t * tok, QT), tok)] = tile_o
        return carry

    lax.fori_loop(0, 4 * nr, tile, 0)

    def odone(ii, carry):
        b, r = tile_of(ii)
        ocopy(b * nr + r, b, r).wait_send()
        remote(osend.at[0], orecv.at[pl.ds(pl.multiple_of(r * QT, QT), QT), pl.ds(pl.multiple_of(b * tok, QT), tok)], o_s.at[0], o_r.at[b, r], tp=b).wait_recv()
        return carry

    lax.fori_loop(0, 3 * nr, odone, 0)
    wofar.wait_send()
    wopart.wait()
    wofwd.wait()

    nt = hid // 4

    def proj_out(n, carry):
        sl = pl.ds(pl.multiple_of(n * nt, QT), nt)
        ow = dot(orecv[...], wo[:, :, sl].reshape(hid, nt))
        h_out[:, sl] = (xh[t, :, sl].astype(F32) + ow).astype(BF16)
        return carry

    lax.fori_loop(0, 4, proj_out, 0)

    def kvdone(b, carry):
        kvcopy(b).wait_send()
        return carry

    lax.fori_loop(0, 4, kvdone, 0)
    for k, (w, wr) in enumerate(((wg, wg_r), (wu, wu_r), (wd, wd_r))):
        remote(w.at[1 - s], wr, ew_s.at[k], ew_r.at[k], tp=part).wait()


def moe_kernel(h, ids, gates, wg, wu, wd, wg_r, wu_r, wd_r,
               y_out,
               g_v, u_v, d_v, send, recv, zsend, zret, zacc,
               w_sem, s_s, s_r, z_s, z_r):
    c = lax.axis_index("cp")
    t = lax.axis_index("tp")
    s = lax.rem(t, 2)
    xx = t // 2
    tok, hid = h.shape
    cap = recv.shape[1]
    nf = g_v.shape[0]
    fw = g_v.shape[2]
    half = nf // 2

    def peer(r):
        return {"cp": lax.rem(c + (r // 2) % 2, 2), "tp": 2 * lax.rem(xx + r // 4, 2) + lax.rem(s + r % 2, 2)}

    def peer_dyn(r):
        return {"cp": lax.rem(c + lax.rem(r // 2, 2), 2), "tp": 2 * lax.rem(xx + r // 4, 2) + lax.rem(s + lax.rem(r, 2), 2)}

    bar = pltpu.get_barrier_semaphore()
    for r in range(1, 8):
        pl.semaphore_signal(bar, inc=1, device_id=peer(r), device_id_type=MESH)

    def wload(f, own):
        if own:
            sl = pl.ds(pl.multiple_of(f * fw, fw), fw)
            srcs = (wg.at[s, :, sl], wu.at[s, :, sl], wd.at[s, sl])
        else:
            sl = pl.ds(pl.multiple_of((f - half) * fw, fw), fw)
            srcs = (wg_r.at[:, sl], wu_r.at[:, sl], wd_r.at[sl])
        return [pltpu.make_async_copy(src, dst.at[f], w_sem.at[k, f]) for k, (src, dst) in enumerate(zip(srcs, (g_v, u_v, d_v)))]

    for f in range(nf):
        for cp_ in wload(f, f < half):
            cp_.start()

    ids_v = ids[...]
    rel = lax.rem(ids_v // 2 + xx, 2) * 4 + lax.rem(ids_v // 4 + c, 2) * 2 + lax.rem(ids_v + s, 2)
    ex_i = lax.broadcasted_iota(jnp.int32, (8, tok), 0)
    oh0 = (rel[0:1] == ex_i).astype(F32)
    oh1 = (rel[1:2] == ex_i).astype(F32)
    before = (lax.broadcasted_iota(jnp.int32, (tok, tok), 0) < lax.broadcasted_iota(jnp.int32, (tok, tok), 1)).astype(F32).astype(BF16)
    cum = dot(jnp.concatenate([oh0, oh1], axis=0).astype(BF16), before)
    base = ex_i.astype(F32) * cap
    tot0 = jnp.sum(oh0, axis=1, keepdims=True)
    slot0 = jnp.sum(oh0 * (base + cum[0:8]), axis=0, keepdims=True)
    slot1 = jnp.sum(oh1 * (base + tot0 + cum[8:16]), axis=0, keepdims=True)

    cap_i = lax.broadcasted_iota(jnp.int32, (cap, tok), 0).astype(F32)

    def block(r):
        want = cap_i + float(r * cap)
        sel = ((slot0 == want) | (slot1 == want)).astype(F32).astype(BF16)
        return dot(sel, h[...]).astype(BF16)

    def scopy(r):
        return remote(send.at[r], recv.at[r], s_s.at[r], s_r.at[r], **peer_dyn(r))

    def zcopy(r):
        return remote(zsend.at[r], zret.at[r], z_s.at[r], z_r.at[r], **peer_dyn(r))

    pl.semaphore_wait(bar, 7)
    for r in (4, 2, 5, 3, 1, 6, 7):
        send[r] = block(r)
        scopy(r).start()
    recv[0] = block(0)

    def group(gi, carry):
        g = lax.rem(gi, 2) * 2 + gi // 2
        @pl.when(gi > 0)
        def _():
            scopy(2 * g).wait_recv()
        scopy(2 * g + 1).wait_recv()
        xg = recv[pl.ds(2 * g, 2)].reshape(2 * cap, hid)
        zacc[...] = jnp.zeros(zacc.shape, F32)

        def fstep(f, cc):
            @pl.when(jnp.logical_and(gi == 0, f < half))
            def _():
                for cp_ in wload(f, True):
                    cp_.wait()

            @pl.when(jnp.logical_and(gi == 0, f >= half))
            def _():
                for cp_ in wload(f, False):
                    cp_.wait()

            gp = dot(xg, g_v[f])
            up = dot(xg, u_v[f])
            a = (jax.nn.silu(gp) * up).astype(BF16)
            zacc[...] += dot(a, d_v[f])
            return cc

        lax.fori_loop(0, nf, fstep, 0)
        z = zacc[...].astype(BF16)

        @pl.when(gi > 0)
        def _():
            zsend[2 * g] = z[:cap]
            zcopy(2 * g).start()

        @pl.when(gi == 0)
        def _():
            zret[0] = z[:cap]

        zsend[2 * g + 1] = z[cap:]
        zcopy(2 * g + 1).start()
        return carry

    lax.fori_loop(0, 4, group, 0)

    cols = jnp.concatenate([slot0, slot1, gates[...], jnp.zeros((4, tok), F32)], axis=0).T
    for r in range(1, 8):
        scopy(r).wait_send()
        zcopy(r).wait()
    slot_i = lax.broadcasted_iota(jnp.int32, (tok, 8 * cap), 1).astype(F32)
    z_all = zret[...].reshape(8 * cap, hid)
    y = h[...].astype(F32)
    for k in range(2):
        sel = (cols[:, k:k + 1] == slot_i).astype(F32).astype(BF16)
        y = y + cols[:, 2 + k:3 + k] * dot(sel, z_all)
    y_out[...] = y.astype(BF16)


def solution(mesh):
    row_spec = P(("dp", "cp", "tp"), None)
    head_spec = P(None, "tp", None)
    expert_spec = P(("cp", "tp"), None, None)
    any_spec = pl.BlockSpec(memory_space=pl.ANY)
    vm = pl.BlockSpec(memory_space=pltpu.VMEM)
    DMA = pltpu.SemaphoreType.DMA

    def device_step(x, w_q, w_k, w_v, w_o, ids, gates, w_gate, w_up, w_down):
        tok, hid = x.shape
        nr = tok // QT
        hd = w_q.shape[1] * w_q.shape[2]
        kd = w_k.shape[1] * w_k.shape[2]
        wq_t = w_q.transpose(1, 2, 0).reshape(hd, hid)
        wk_t = w_k.transpose(1, 2, 0).reshape(kd, hid)
        wv_t = w_v.transpose(1, 2, 0).reshape(kd, hid)
        wo = w_o.reshape(hd, hid)
        seq = 8 * tok
        npair = w_q.shape[1] // 2
        f = w_gate.shape[2]

        h, wg_r, wu_r, wd_r = pl.pallas_call(
            attn_kernel,
            out_shape=[
                jax.ShapeDtypeStruct((tok, hid), BF16),
                jax.ShapeDtypeStruct((hid, f), BF16),
                jax.ShapeDtypeStruct((hid, f), BF16),
                jax.ShapeDtypeStruct((f, hid), BF16),
            ],
            in_specs=[any_spec] * 8,
            out_specs=[vm, any_spec, any_spec, any_spec],
            scratch_shapes=[
                pltpu.VMEM((4, tok, hid), BF16),
                pltpu.VMEM((hd, hid), BF16),
                pltpu.VMEM((2 * kd, hid), BF16),
                pltpu.VMEM((4, hd, hid), BF16),
                pltpu.VMEM((4, 2 * kd, tok), BF16),
                pltpu.VMEM((4, 2 * kd, tok), BF16),
                pltpu.VMEM((2, seq, 128), BF16),
                pltpu.VMEM((kd, seq), BF16),
                pltpu.VMEM((4 * nr, npair, 128, 2 * QT), BF16),
                pltpu.VMEM((4 * nr, QT, hd), BF16),
                pltpu.VMEM((tok, 4 * hd), BF16),
                pltpu.VMEM((npair, 1, 2 * QT), F32),
                pltpu.VMEM((npair, 8, 2 * QT), F32),
                pltpu.VMEM((npair, 32, 2 * QT), F32),
                DMA((5,)), DMA((nr,)), DMA((nr,)), DMA, DMA, DMA((nr,)), DMA((nr,)),
                DMA((4,)), DMA((4,)), DMA((3,)), DMA((3,)), DMA((3,)), DMA((3,)),
                DMA((4 * nr,)), DMA((4, nr)),
            ],
            compiler_params=pltpu.CompilerParams(collective_id=0, has_side_effects=True, vmem_limit_bytes=60 * 1024 * 1024),
            name="attn",
        )(x, wq_t, wk_t, wv_t, wo, w_gate, w_up, w_down)

        cap = tok * 2 // 8
        fw = f // 4
        return pl.pallas_call(
            moe_kernel,
            out_shape=jax.ShapeDtypeStruct((tok, hid), BF16),
            in_specs=[vm, vm, vm] + [any_spec] * 6,
            out_specs=vm,
            scratch_shapes=[
                pltpu.VMEM((8, hid, fw), BF16),
                pltpu.VMEM((8, hid, fw), BF16),
                pltpu.VMEM((8, fw, hid), BF16),
                pltpu.VMEM((8, cap, hid), BF16),
                pltpu.VMEM((8, cap, hid), BF16),
                pltpu.VMEM((8, cap, hid), BF16),
                pltpu.VMEM((8, cap, hid), BF16),
                pltpu.VMEM((2 * cap, hid), F32),
                DMA((3, 8)), DMA((8,)), DMA((8,)), DMA((8,)), DMA((8,)),
            ],
            compiler_params=pltpu.CompilerParams(collective_id=1, has_side_effects=True, vmem_limit_bytes=63 * 1024 * 1024),
            name="moe",
        )(h, ids.T, gates.T, w_gate, w_up, w_down, wg_r, wu_r, wd_r)

    return jax.shard_map(device_step, mesh=mesh, in_specs=(row_spec, head_spec, head_spec, head_spec, P("tp", None, None), row_spec, row_spec, expert_spec, expert_spec, expert_spec), out_specs=row_spec, check_vma=False)
```

time: 696 us -> 252 us (0.36); the launches traced: 689 us -> 252 us
  Pallas kernels: 0 us -> 249 us
  matrix products: 234 us -> 0 us
  waiting for transfers between devices: 186 us -> 0 us
  other arithmetic: 119 us -> 0 us
  blocking collectives: 87.2 us -> 0 us
  local copies, waits for them, and re-layouts: 36.2 us -> 2.36 us
  between operations: 14.2 us -> 0.02 us
  starting transfers between devices: 12.6 us -> 0 us
    pallas_call x0 -> x2, Pallas kernels: none -> 249 us  [the longest x1 180 us: device_step(): pl.pallas_call(attn_kernel, out_shape=[jax.ShapeDtypeStruct((tok, hid), B...]
    dot_general x8 -> x0, matrix products: 226 us -> none  [the longest x2 84.7 us: attend_block(): jnp.einsum('qgrd,kgd->grqk', q_loc, k_blk, preferred_element_type=jnp.flo...]
    reduce_sum x3 -> x0, other arithmetic: 95.1 us -> none  [the longest x1 71.8 us: attend_block(): new_sum = run_sum * rescale + jnp.sum(prob_vals, axis=-1)]
    all_to_all x2 -> x0, blocking collectives: 87.2 us -> none  [the longest x1 56.3 us: device_step(): recv_buf = lax.all_to_all(send_buf, 'tp', 1, 1, tiled=True)]
    all_to_all x2 -> x0, waiting for transfers between devices: 80.1 us -> none  [the longest x1 52.6 us: device_step(): recv_buf = lax.all_to_all(recv_buf, 'cp', 0, 0, tiled=True)]
    reduce_scatter x1 -> x0, waiting for transfers between devices: 61.5 us -> none  [device_step(): lax.psum_scatter(attn_part, 'tp', scatter_dimension=0, tiled=True)]
    all_gather x1 -> x0, waiting for transfers between devices: 35.4 us -> none  [device_step(): x_half = lax.all_gather(x_loc, 'tp', axis=0, tiled=True)]
    gather x3 -> x0, local copies, waits for them, and re-layouts: 17.5 us -> none  [the longest x2 13.7 us: device_step(): picked = jnp.take(z_full, dest_idx, axis=0).reshape(tok_dev, top_k, hid_dim)]
  transfers between devices with their start and end apart: 7 -> 0, of which waited for: 5 -> 0; matrix products, arithmetic and copies ran while one was open for 31% -> 0% of each run, Pallas kernels for 0% -> 0%
where the time goes in v1:
time: 252 us
  Pallas kernels  249 us (99%)
    pallas_call x1, Pallas kernels, device_step(): pl.pallas_call(attn_kernel, out_shape=[jax.ShapeDtypeStruct((tok, hid), B...  180 us
    pallas_call x1, Pallas kernels, device_step(): pl.pallas_call(moe_kernel, out_shape=jax.ShapeDtypeStruct((tok, hid), BF1...  69.1 us

profile of v1, /device:TPU:0, one launch (start us, length us, event | category | flops | bytes accessed | tf_op | source)
XLA Modules:
  0.0 251.7 jit_solution(10839148275109511316)
XLA Ops:
  0.0 180.3 %attn.1 = (bf16[384,1536]{1,0:T(8,128)(2,1)}, bf16[1536,2048]{1,0:T(8,128)(2,1)}, bf16[1536,2048]{1,0:T(8,128)(2,1)}, bf16[2048,1536]{1,0:T(8,128)(2,1)}) custom-call(bf16[384,1536]{1,0:T(8,128)(2,1)} %x.1, bf16[384,1536]{1,0:T(8,128)(2,1)} %bitcast.12, bf16[64,1536]{1,0:T(8,128)(2,1)} %bitcast.14, bf16[64,1536]{1,0:T(8,128)(2,1)} %bitcast.15, ...), custom_call_target="tpu_custom_call" | custom-call | tf_op jit(solution)/shard_map/attn/pallas_call | solution.py:416
  180.3 69.1 %moe.1 = bf16[384,1536]{1,0:T(8,128)(2,1)} custom-call(bf16[384,1536]{1,0:T(8,128)(2,1)} %get-tuple-element.9.h, s32[2,384]{1,0:T(2,128)} %bitcast.16, f32[2,384]{1,0:T(2,128)} %bitcast.17, bf16[2,1536,2048]{2,1,0:T(8,128)(2,1)} %wg.3, bf16[2,1536,2048]{2,1,0:T(8,128)(2,1)} %wu.3, bf16[2,2048,1536]{2,1,0:T(8,128)(2,1)} %wd.3, ...), custom_call_target="tpu_custom_call" | custom-call | tf_op jit(solution)/shard_map/moe/pallas_call | solution.py:451
  249.3 2.4 copy.12

commit v2 on v1

--- a/solution.py
+++ b/solution.py
@@ -31,7 +31,7 @@
 
 def attn_kernel(x, wq_h, wk_h, wv_h, wo_h, wg, wu, wd,
                 h_out, wg_r, wu_r, wd_r,
-                xh, wq, wkv, wo, kvown, kvrecv, kaug, vt, qaug, osend, orecv, m_s, l_s, acc_s,
+                xh, wq, wkv, wo, kvown, kvrecv, kaug, vt, qaug, osend, orecv, m_s, l_s, acc_s, s_s, mx_s,
                 loc_sem, xf_s, xf_r, xp_s, xp_r, xw_s, xw_r, kv_s, kv_r, wo_s, wo_r, ew_s, ew_r, o_s, o_r):
     c = lax.axis_index("cp")
     t = lax.axis_index("tp")
@@ -167,6 +167,18 @@
         sl = pl.ds(pl.multiple_of(ii * n, n), n)
         return remote(wd.at[1 - s, sl], wd_r.at[sl], ew_s.at[2], ew_r.at[2], tp=part)
 
+    def fold_max(v):
+        return jnp.max(v.reshape(KC // 8, 8, 2 * QT), axis=0)
+
+    def score(p, i, j):
+        return dot(kaug[p // (npair // 2), pl.ds(pl.multiple_of(j * KC, KC), KC), :], qaug[i, p])
+
+    b0, r0 = tile_of(0)
+    for p in range(npair):
+        s_first = score(p, b0 * nr + r0, 0)
+        s_s[p] = s_first
+        mx_s[p] = fold_max(s_first)
+
     def tile(ii, carry):
         for cp_ in wcopy(ii):
             cp_.start()
@@ -190,7 +202,7 @@
         l_s[...] = jnp.zeros(l_s.shape, F32)
         acc_s[...] = jnp.zeros(acc_s.shape, F32)
 
-        def step(j, masked):
+        def step(j, i_next, j_next, masked):
             k0 = pl.multiple_of(j * KC, KC)
             if masked:
                 key_i = lax.broadcasted_iota(jnp.int32, (KC, 2 * QT), 0) + k0
@@ -198,26 +210,31 @@
                 allowed = key_i <= q_i
             for p in range(npair):
                 g = p // (npair // 2)
-                sc = dot(kaug[g, pl.ds(k0, KC), :], qaug[i, p])
+                s_next = score(p, i_next, j_next)
+                sc = s_s[p]
                 if masked:
                     sc = jnp.where(allowed, sc, -jnp.inf)
-                s8 = sc.reshape(KC // 8, 8, 2 * QT)
-                mx = jnp.max(jnp.max(s8, axis=0), axis=0, keepdims=True)
+                    mx = fold_max(sc)
+                else:
+                    mx = mx_s[p]
                 m_old = m_s[p]
-                m_new = jnp.maximum(m_old, mx)
+                m_new = jnp.maximum(m_old, jnp.max(mx, axis=0, keepdims=True))
                 alpha = jnp.exp2(m_old - m_new)
                 pr = jnp.exp2(sc - m_new)
                 l_s[p] = l_s[p] * alpha + jnp.sum(pr.reshape(KC // 8, 8, 2 * QT), axis=0)
                 pv = dot(vt[g * 32:(g + 1) * 32, pl.ds(k0, KC)], pr.astype(BF16))
                 acc_s[p] = acc_s[p] * alpha + pv
                 m_s[p] = m_new
+                s_s[p] = s_next
+                mx_s[p] = fold_max(s_next)
 
         def body(j, cc):
-            step(j, False)
+            step(j, i, j + 1, False)
             return cc
 
         lax.fori_loop(0, nfull, body, 0)
-        step(nfull, True)
+        bn, rn = tile_of(jnp.minimum(ii + 1, 4 * nr - 1))
+        step(nfull, bn * nr + rn, 0, True)
 
         pieces = []
         for p in range(npair):
@@ -438,6 +455,8 @@
                 pltpu.VMEM((npair, 1, 2 * QT), F32),
                 pltpu.VMEM((npair, 8, 2 * QT), F32),
                 pltpu.VMEM((npair, 32, 2 * QT), F32),
+                pltpu.VMEM((npair, KC, 2 * QT), F32),
+                pltpu.VMEM((npair, 8, 2 * QT), F32),
                 DMA((5,)), DMA((nr,)), DMA((nr,)), DMA, DMA, DMA((nr,)), DMA((nr,)),
                 DMA((4,)), DMA((4,)), DMA((3,)), DMA((3,)), DMA((3,)), DMA((3,)),
                 DMA((4 * nr,)), DMA((4, nr)),

time: 252 us -> 167 us (0.66)
  Pallas kernels: 249 us -> 164 us
    pallas_call x1, Pallas kernels: 180 us -> 84.5 us  [device_step(): pl.pallas_call(attn_kernel, out_shape=[jax.ShapeDtypeStruct((tok, hid), B...]
    pallas_call x1, Pallas kernels: 69.1 us -> 79.9 us  [device_step(): pl.pallas_call(moe_kernel, out_shape=jax.ShapeDtypeStruct((tok, hid), BF1...]
where the time goes in v2:
time: 167 us
  Pallas kernels  164 us (98%)
  local copies, waits for them, and re-layouts  2.36 us (1%)
    pallas_call x1, Pallas kernels, device_step(): pl.pallas_call(attn_kernel, out_shape=[jax.ShapeDtypeStruct((tok, hid), B...  84.5 us
    pallas_call x1, Pallas kernels, device_step(): pl.pallas_call(moe_kernel, out_shape=jax.ShapeDtypeStruct((tok, hid), BF1...  79.9 us

profile of v2, /device:TPU:0, one launch (start us, length us, event | category | flops | bytes accessed | tf_op | source)
XLA Modules:
  0.0 166.8 jit_solution(18362853711243450721)
XLA Ops:
  0.0 84.5 %attn.1 = (bf16[384,1536]{1,0:T(8,128)(2,1)}, bf16[1536,2048]{1,0:T(8,128)(2,1)}, bf16[1536,2048]{1,0:T(8,128)(2,1)}, bf16[2048,1536]{1,0:T(8,128)(2,1)}) custom-call(bf16[384,1536]{1,0:T(8,128)(2,1)} %x.1, bf16[384,1536]{1,0:T(8,128)(2,1)} %bitcast.12, bf16[64,1536]{1,0:T(8,128)(2,1)} %bitcast.14, bf16[64,1536]{1,0:T(8,128)(2,1)} %bitcast.15, ...), custom_call_target="tpu_custom_call" | custom-call | tf_op jit(solution)/shard_map/attn/pallas_call | solution.py:433
  84.5 79.9 %moe.1 = bf16[384,1536]{1,0:T(8,128)(2,1)} custom-call(bf16[384,1536]{1,0:T(8,128)(2,1)} %get-tuple-element.9.h, s32[2,384]{1,0:T(2,128)} %bitcast.16, f32[2,384]{1,0:T(2,128)} %bitcast.17, bf16[2,1536,2048]{2,1,0:T(8,128)(2,1)} %wg.3, bf16[2,1536,2048]{2,1,0:T(8,128)(2,1)} %wu.3, bf16[2,2048,1536]{2,1,0:T(8,128)(2,1)} %wd.3, ...), custom_call_target="tpu_custom_call" | custom-call | tf_op jit(solution)/shard_map/moe/pallas_call | solution.py:470
  164.4 2.4 %copy.12 = bf16[384,1536]{1,0:T(8,128)(2,1)} copy(bf16[384,1536]{1,0:T(8,128)(2,1)} %moe.1) | data formatting | bytes 2359296

commit v3 on v2

v3 whole, which is shorter than its diff:
```python
import functools
import math

import jax
import jax.numpy as jnp
from jax import lax
from jax.experimental import pallas as pl
from jax.experimental.pallas import tpu as pltpu
from jax.sharding import PartitionSpec as P

MESH = pl.DeviceIdType.MESH
F32 = jnp.float32
BF16 = jnp.bfloat16

NT = (((1,), (1,)), ((), ()))
QT = 128
KC = 256


def dot(a, b):
    return jnp.dot(a, b, preferred_element_type=F32)


def dot_nt(a, b):
    return lax.dot_general(a, b, NT, preferred_element_type=F32)


def remote(src, dst, send, recv, **dev):
    return pltpu.make_async_remote_copy(src_ref=src, dst_ref=dst, send_sem=send, recv_sem=recv, device_id=dev, device_id_type=MESH)


def attn_kernel(x, wq_h, wk_h, wv_h, wo_h, wg, wu, wd,
                h_out, wg_r, wu_r, wd_r,
                xh, wq, wkv, wo, kvown, kvrecv, kaug, vt, qaug, osend, orecv, m_s, l_s, acc_s, s_s, mx_s,
                loc_sem, xf_s, xf_r, xp_s, xp_r, xw_s, xw_r, kv_s, kv_r, wo_s, wo_r, ew_s, ew_r, o_s, o_r):
    c = lax.axis_index("cp")
    t = lax.axis_index("tp")
    s = lax.rem(t, 2)
    xx = t // 2
    part = t + 1 - 2 * s
    far = lax.rem(t + 2, 4)
    farp = lax.rem(part + 2, 4)
    cn = 1 - c
    tok, hid = x.shape
    nr = tok // QT
    nt = 2 * nr
    nk = 2 * tok // KC
    heads = wq_h.shape[0] // 32
    npair = heads // 2
    scale = 32 ** -0.5 * math.log2(math.e)

    lc = c + xx * (3 - 2 * c)
    rc = 3 - lc
    ln = cn + xx * (3 - 2 * cn)
    rn = 3 - ln
    pp = lax.rem(xx + c, 2)
    qq = 1 - pp

    bar = pltpu.get_barrier_semaphore()
    pl.semaphore_signal(bar, inc=1, device_id={"tp": part}, device_id_type=MESH)
    pl.semaphore_signal(bar, inc=1, device_id={"tp": far}, device_id_type=MESH)
    pl.semaphore_signal(bar, inc=1, device_id={"tp": farp}, device_id_type=MESH)
    pl.semaphore_signal(bar, inc=1, device_id={"cp": cn}, device_id_type=MESH)

    own_rows = pl.ds(pl.multiple_of(s * tok, QT), tok)
    locs = [
        pltpu.make_async_copy(x, xh.at[0, own_rows], loc_sem.at[0]),
        pltpu.make_async_copy(wq_h, wq, loc_sem.at[1]),
        pltpu.make_async_copy(wk_h, wkv.at[pl.ds(0, 64)], loc_sem.at[2]),
        pltpu.make_async_copy(wv_h, wkv.at[pl.ds(64, 64)], loc_sem.at[3]),
        pltpu.make_async_copy(wo_h, wo.at[t], loc_sem.at[4]),
    ]
    for cp_ in locs:
        cp_.start()
    pl.semaphore_wait(bar, 4)

    def piece(k, who):
        return pl.ds(pl.multiple_of((2 * k + who) * QT, QT), QT)

    def xfar(k):
        return remote(xh.at[0, piece(k, s)], xh.at[1, piece(k, s)], xf_s.at[k], xf_r.at[k], tp=far)

    def xfwd(k):
        return remote(xh.at[1, piece(k, s)], xh.at[1, piece(k, s)], xw_s.at[k], xw_r.at[k], tp=part)

    def xfwd_in(k):
        return remote(xh.at[1, piece(k, s)], xh.at[1, piece(k, 1 - s)], xw_s.at[k], xw_r.at[k], tp=part)

    hw = wo.shape[1] // 4

    def wo_rows(cc, n):
        return pl.ds(pl.multiple_of((2 * cc + n) * hw, hw), hw)

    def wofar(n):
        return remote(wo_h.at[wo_rows(c, n)], wo.at[t, wo_rows(c, n)], wo_s.at[n], wo_r.at[n], tp=far)

    def woy(n):
        return remote(wo.at[far, wo_rows(c, n)], wo.at[far, wo_rows(c, n)], wo_s.at[2 + n], wo_r.at[2 + n], cp=cn)

    def wofwd(n):
        return remote(wo.at[far, wo_rows(c, n)], wo.at[far, wo_rows(c, n)], wo_s.at[4 + n], wo_r.at[4 + n], tp=part)

    def wofwdy(n):
        return remote(wo.at[far, wo_rows(cn, n)], wo.at[far, wo_rows(cn, n)], wo_s.at[6 + n], wo_r.at[6 + n], tp=part)

    xpart = remote(x, xh.at[0, own_rows], xp_s, xp_r, tp=part)
    xpart.start()
    locs[0].wait()

    @pl.when(s == 0)
    def _():
        xfar(0).start()
        xfar(1).start()

    qaug[:, :, 96:128, :] = jnp.zeros((qaug.shape[0], npair, 32, 2 * QT), BF16)
    kaug[:, :, 96:128] = jnp.zeros((2, kaug.shape[1], 32), BF16)
    m_s[...] = jnp.full(m_s.shape, -jnp.inf, F32)
    l_s[...] = jnp.zeros(l_s.shape, F32)
    acc_s[...] = jnp.zeros(acc_s.shape, F32)

    zero_pad = jnp.zeros((32, KC), BF16)

    def place(kv, ck, k):
        pos = pl.multiple_of((ck * nk + k) * KC, KC)
        for g in range(2):
            kt = kv[g * 32:(g + 1) * 32]
            kaug[g, pl.ds(pos, KC), :] = jnp.concatenate([kt, kt, kt, zero_pad], axis=0).T
        vt[:, pl.ds(pos, KC)] = kv[64:128]

    def kvcopy(side, k):
        return remote(kvown.at[side, k], kvrecv.at[side, k], kv_s.at[side, k], kv_r.at[side, k], cp=cn)

    def project(side, k):
        xb = xh[side, pl.ds(pl.multiple_of(k * KC, KC), KC), :]
        kv = dot_nt(wkv[...], xb).astype(BF16)
        kvown[side, k] = kv
        kvcopy(side, k).start()
        place(kv, lc + side * (rc - lc), k)
        qt = dot_nt(wq[...], xb).astype(BF16)
        qs = qt.astype(F32) * scale
        h1 = qs.astype(BF16)
        r1 = qs - h1.astype(F32)
        h2 = r1.astype(BF16)
        h3 = (r1 - h2.astype(F32)).astype(BF16)
        for r in range(2):
            for hd in range(heads):
                for n, part_v in enumerate((h1, h2, h3)):
                    qaug[side * nt + 2 * k + r, hd // 2, n * 32:(n + 1) * 32, (hd % 2) * QT:(hd % 2 + 1) * QT] = part_v[hd * 32:(hd + 1) * 32, r * QT:(r + 1) * QT]

    for cp_ in locs[1:4]:
        cp_.wait()
    xpart.wait_recv()

    @pl.when(s == 1)
    def _():
        xfar(0).start()
        xfar(1).start()

    xfar(2).start()
    for n in range(2):
        wofar(n).start()

    def project_own(k, carry):
        project(0, k)
        return carry

    lax.fori_loop(0, nk, project_own, 0)

    wopart = remote(wo_h, wo.at[t], wo_s.at[8], wo_r.at[8], tp=part)
    wopart.start()

    e0 = 2 * nt + 3 * nt * pp
    e1 = e0 + 14 + 2 * qq
    e2 = e1 + 16 + 6 * qq
    njob = 78
    w0 = 8
    w1 = 60

    def pick(*pairs):
        out = pairs[-1][1]
        for cond, val in reversed(pairs[:-1]):
            out = jnp.where(cond, val, out)
        return out

    def job(i):
        k1 = pick((i < 2, 0), (i < 6, 1), (None, 2))
        v1 = i - k1 * (k1 + 1)
        v2 = i - 2 * nt
        k = pick((i < e1, 0), (i < e2, 1), (None, 2))
        u = i - pick((i < e1, e0), (i < e2, e1), (None, e2))
        nc2 = qq * 2 * k
        ua = jnp.where(u < 6, u, u - nc2)
        ub = u - 12 - nc2
        uc = ub - 2 * (k + 1)
        in1 = i < 2 * nt
        in2 = i < e0
        in_c2 = jnp.logical_and(u >= 6, u < 6 + nc2)
        in_a = u < 12 + nc2
        in_b = ub < 2 * (k + 1)
        first = xx == 0
        slot_a = jnp.where(first, nt + 2 * k + ua // 6, lax.rem(jnp.maximum(ua, 0), 6))
        ch_a = jnp.where(first, jnp.where(lax.rem(jnp.maximum(ua, 0), 6) < 3, lc, ln) * nk + lax.rem(jnp.maximum(ua, 0), 3), jnp.where(ua < 6, rc, rn) * nk + k)
        ubp = jnp.maximum(ub, 0)
        ucp = jnp.maximum(uc, 0)
        v2p = jnp.maximum(v2, 0)
        slot = pick((in1, 2 * k1 + lax.rem(jnp.maximum(v1, 0), 2)), (in2, v2p // 3), (in_c2, nt + u - 6), (in_a, slot_a), (in_b, nt + 2 * k + lax.rem(ubp, 2)), (None, nt + 2 * k + lax.rem(ucp, 2)))
        ch = pick((in1, lc * nk + v1 // 2), (in2, ln * nk + lax.rem(v2p, 3)), (in_c2, rn * nk + k), (in_a, ch_a), (in_b, rc * nk + ubp // 2), (None, rn * nk + ucp // 2))
        one, zero = jnp.int32(1), jnp.int32(0)
        masked = pick((in1, jnp.where(v1 // 2 == k1, one, zero)), (in2, zero), (in_a, zero), (in_b, jnp.where(ubp // 2 == k, one, zero)), (None, zero))
        last = jnp.where(k == 2, one, zero)
        fin = pick((in1, masked * (1 - xx) * qq), (in2, jnp.where(lax.rem(v2p, 3) == 2, 1 - xx, zero)), (in_c2, last), (in_a, last * xx * jnp.where(ua >= 6, one, zero)), (in_b, masked * pp), (None, last * jnp.where(ucp // 2 == 2, one, zero)))
        return slot, ch, masked, fin

    def fold_max(v):
        return jnp.max(v.reshape(KC // 8, 8, 2 * QT), axis=0)

    def score(p, slot, ch):
        return dot(kaug[p // (npair // 2), pl.ds(pl.multiple_of(ch * KC, KC), KC), :], qaug[slot, p])

    for p in range(npair):
        s_first = score(p, 0, lc * nk)
        s_s[p] = s_first
        mx_s[p] = fold_max(s_first)

    def wcopy(k, ii, n):
        w, wr = ((wg, wg_r), (wu, wu_r), (wd, wd_r))[k]
        sl = pl.ds(pl.multiple_of(ii * n, n), n)
        return remote(w.at[1 - s, sl], wr.at[sl], ew_s.at[k], ew_r.at[k], tp=part)

    def ocopy(slot, b, r):
        return remote(osend.at[slot], orecv.at[pl.ds(pl.multiple_of(r * QT, QT), QT), pl.ds(pl.multiple_of(t * tok, QT), tok)], o_s.at[slot], o_r.at[t, r], tp=b)

    def where_of(slot):
        u = lax.rem(slot, nt)
        chip = lax.rem(xx + slot // nt, 2)
        return 2 * chip + u // nr, lax.rem(u, nr)

    def step(i, carry):
        (slot, ch, masked, fin), following = carry
        slot_n, ch_n = following[:2]
        k_ev = pick((i < e1 - 1, 0), (i < e2 - 1, 1), (None, 2))
        e_ev = pick((i < e1 - 1, e0), (i < e2 - 1, e1), (None, e2))

        @pl.when(i == 2 * nt - 1)
        def _():
            def take(k, cc):
                kvcopy(0, k).wait_recv()
                place(kvrecv[0, k], ln, k)
                return cc
            lax.fori_loop(0, nk, take, 0)

        @pl.when(i == e_ev - 1)
        def _():
            xfar(k_ev).wait_recv()
            xfwd(k_ev).start()
            xfwd_in(k_ev).wait_recv()
            project(1, k_ev)

        @pl.when(i == w1)
        def _():
            locs[4].wait()
            for n in range(2):
                wofar(n).wait_recv()
                woy(n).start()
                wofwd(n).start()

        k_r = pick((i < e1, 0), (i < e2, 1), (None, 2))
        e_r = pick((i < e1, e0), (i < e2, e1), (None, e2))

        @pl.when(i == e_r + 5)
        def _():
            kvcopy(1, k_r).wait_recv()
            place(kvrecv[1, k_r], rn, k_r)

        wi = i - w0

        @pl.when(jnp.logical_and(wi >= 0, wi < 64))
        def _():
            wcopy(2, wi, wd.shape[1] // 64).start()

            @pl.when(lax.rem(wi, 2) == 0)
            def _():
                wcopy(0, wi // 2, wg.shape[1] // 32).start()

            @pl.when(lax.rem(wi, 2) == 1)
            def _():
                wcopy(1, wi // 2, wu.shape[1] // 32).start()

        @pl.when(masked == 1)
        def _():
            qpos = ((lc + (slot // nt) * (rc - lc)) * nt + lax.rem(slot, nt)) * QT
            key_i = lax.broadcasted_iota(jnp.int32, (KC, 2 * QT), 0) + ch * KC
            q_i = lax.rem(lax.broadcasted_iota(jnp.int32, (KC, 2 * QT), 1), QT) + qpos
            allowed = key_i <= q_i
            for p in range(npair):
                sc = jnp.where(allowed, s_s[p], -jnp.inf)
                s_s[p] = sc
                mx_s[p] = fold_max(sc)

        after = job(jnp.minimum(i + 2, njob - 1))
        k0 = pl.multiple_of(ch * KC, KC)
        for p in range(npair):
            g = p // (npair // 2)
            s_next = score(p, slot_n, ch_n)
            sc = s_s[p]
            m_old = m_s[slot, p]
            m_new = jnp.maximum(m_old, jnp.max(mx_s[p], axis=0, keepdims=True))
            alpha = jnp.exp2(m_old - m_new)
            pr = jnp.exp2(sc - m_new)
            l_s[slot, p] = l_s[slot, p] * alpha + jnp.sum(pr.reshape(KC // 8, 8, 2 * QT), axis=0)
            pv = dot(vt[g * 32:(g + 1) * 32, pl.ds(k0, KC)], pr.astype(BF16))
            acc_s[slot, p] = acc_s[slot, p] * alpha + pv
            m_s[slot, p] = m_new
            s_s[p] = s_next
            mx_s[p] = fold_max(s_next)

        @pl.when(fin == 1)
        def _():
            pieces = []
            for p in range(npair):
                o = acc_s[slot, p] / jnp.sum(l_s[slot, p], axis=0, keepdims=True)
                pieces += [o[:, :QT], o[:, QT:]]
            tile_o = jnp.concatenate(pieces, axis=0).T.astype(BF16)
            b, r = where_of(slot)

            @pl.when(b != t)
            def _():
                osend[slot] = tile_o
                ocopy(slot, b, r).start()

            @pl.when(b == t)
            def _():
                orecv[pl.ds(pl.multiple_of(r * QT, QT), QT), pl.ds(pl.multiple_of(t * tok, QT), tok)] = tile_o
        return following, after

    lax.fori_loop(0, njob, step, (job(jnp.int32(0)), job(jnp.int32(1))))

    for n in range(2):
        woy(n).wait_recv()
        wofwdy(n).start()

    def odone(slot, carry):
        b, r = where_of(slot)

        @pl.when(b != t)
        def _():
            ocopy(slot, b, r).wait_send()
            remote(osend.at[0], orecv.at[pl.ds(pl.multiple_of(r * QT, QT), QT), pl.ds(pl.multiple_of(b * tok, QT), tok)], o_s.at[0], o_r.at[b, r], tp=b).wait_recv()
        return carry

    lax.fori_loop(0, 2 * nt, odone, 0)
    wopart.wait()
    for n in range(2):
        wofar(n).wait_send()
        woy(n).wait_send()
        wofwd(n).wait()
        wofwdy(n).wait()

    nw = hid // 4

    def proj_out(n, carry):
        sl = pl.ds(pl.multiple_of(n * nw, QT), nw)
        ow = dot(orecv[...], wo[:, :, sl].reshape(hid, nw))
        h_out[:, sl] = (xh[0, own_rows, sl].astype(F32) + ow).astype(BF16)
        return carry

    lax.fori_loop(0, 4, proj_out, 0)

    def drain(k, carry):
        kvcopy(0, k).wait_send()
        kvcopy(1, k).wait_send()
        xfar(k).wait_send()
        xfwd(k).wait_send()
        return carry

    lax.fori_loop(0, nk, drain, 0)
    xpart.wait_send()
    for k, (w, wr) in enumerate(((wg, wg_r), (wu, wu_r), (wd, wd_r))):
        remote(w.at[1 - s], wr, ew_s.at[k], ew_r.at[k], tp=part).wait()


def moe_kernel(h, ids, gates, wg, wu, wd, wg_r, wu_r, wd_r,
               y_out,
               g_v, u_v, d_v, send, recv, zsend, zret, zacc,
               w_sem, s_s, s_r, z_s, z_r):
    c = lax.axis_index("cp")
    t = lax.axis_index("tp")
    s = lax.rem(t, 2)
    xx = t // 2
    tok, hid = h.shape
    cap = recv.shape[1]
    nf = g_v.shape[0]
    fw = g_v.shape[2]
    half = nf // 2

    def peer(r):
        return {"cp": lax.rem(c + (r // 2) % 2, 2), "tp": 2 * lax.rem(xx + r // 4, 2) + lax.rem(s + r % 2, 2)}

    def peer_dyn(r):
        return {"cp": lax.rem(c + lax.rem(r // 2, 2), 2), "tp": 2 * lax.rem(xx + r // 4, 2) + lax.rem(s + lax.rem(r, 2), 2)}

    bar = pltpu.get_barrier_semaphore()
    for r in range(1, 8):
        pl.semaphore_signal(bar, inc=1, device_id=peer(r), device_id_type=MESH)

    def wload(f, own):
        if own:
            sl = pl.ds(pl.multiple_of(f * fw, fw), fw)
            srcs = (wg.at[s, :, sl], wu.at[s, :, sl], wd.at[s, sl])
        else:
            sl = pl.ds(pl.multiple_of((f - half) * fw, fw), fw)
            srcs = (wg_r.at[:, sl], wu_r.at[:, sl], wd_r.at[sl])
        return [pltpu.make_async_copy(src, dst.at[f], w_sem.at[k, f]) for k, (src, dst) in enumerate(zip(srcs, (g_v, u_v, d_v)))]

    for f in range(nf):
        for cp_ in wload(f, f < half):
            cp_.start()

    ids_v = ids[...]
    rel = lax.rem(ids_v // 2 + xx, 2) * 4 + lax.rem(ids_v // 4 + c, 2) * 2 + lax.rem(ids_v + s, 2)
    ex_i = lax.broadcasted_iota(jnp.int32, (8, tok), 0)
    oh0 = (rel[0:1] == ex_i).astype(F32)
    oh1 = (rel[1:2] == ex_i).astype(F32)
    before = (lax.broadcasted_iota(jnp.int32, (tok, tok), 0) < lax.broadcasted_iota(jnp.int32, (tok, tok), 1)).astype(F32).astype(BF16)
    cum = dot(jnp.concatenate([oh0, oh1], axis=0).astype(BF16), before)
    base = ex_i.astype(F32) * cap
    tot0 = jnp.sum(oh0, axis=1, keepdims=True)
    slot0 = jnp.sum(oh0 * (base + cum[0:8]), axis=0, keepdims=True)
    slot1 = jnp.sum(oh1 * (base + tot0 + cum[8:16]), axis=0, keepdims=True)

    cap_i = lax.broadcasted_iota(jnp.int32, (cap, tok), 0).astype(F32)

    def block(r):
        want = cap_i + float(r * cap)
        sel = ((slot0 == want) | (slot1 == want)).astype(F32).astype(BF16)
        return dot(sel, h[...]).astype(BF16)

    def scopy(r):
        return remote(send.at[r], recv.at[r], s_s.at[r], s_r.at[r], **peer_dyn(r))

    def zcopy(r):
        return remote(zsend.at[r], zret.at[r], z_s.at[r], z_r.at[r], **peer_dyn(r))

    pl.semaphore_wait(bar, 7)
    for r in (4, 2, 5, 3, 1, 6, 7):
        send[r] = block(r)
        scopy(r).start()
    recv[0] = block(0)

    def group(gi, carry):
        g = lax.rem(gi, 2) * 2 + gi // 2
        @pl.when(gi > 0)
        def _():
            scopy(2 * g).wait_recv()
        scopy(2 * g + 1).wait_recv()
        xg = recv[pl.ds(2 * g, 2)].reshape(2 * cap, hid)
        zacc[...] = jnp.zeros(zacc.shape, F32)

        def fstep(f, cc):
            @pl.when(jnp.logical_and(gi == 0, f < half))
            def _():
                for cp_ in wload(f, True):
                    cp_.wait()

            @pl.when(jnp.logical_and(gi == 0, f >= half))
            def _():
                for cp_ in wload(f, False):
                    cp_.wait()

            gp = dot(xg, g_v[f])
            up = dot(xg, u_v[f])
            a = (jax.nn.silu(gp) * up).astype(BF16)
            zacc[...] += dot(a, d_v[f])
            return cc

        lax.fori_loop(0, nf, fstep, 0)
        z = zacc[...].astype(BF16)

        @pl.when(gi > 0)
        def _():
            zsend[2 * g] = z[:cap]
            zcopy(2 * g).start()

        @pl.when(gi == 0)
        def _():
            zret[0] = z[:cap]

        zsend[2 * g + 1] = z[cap:]
        zcopy(2 * g + 1).start()
        return carry

    lax.fori_loop(0, 4, group, 0)

    cols = jnp.concatenate([slot0, slot1, gates[...], jnp.zeros((4, tok), F32)], axis=0).T
    for r in range(1, 8):
        scopy(r).wait_send()
        zcopy(r).wait()
    slot_i = lax.broadcasted_iota(jnp.int32, (tok, 8 * cap), 1).astype(F32)
    z_all = zret[...].reshape(8 * cap, hid)
    y = h[...].astype(F32)
    for k in range(2):
        sel = (cols[:, k:k + 1] == slot_i).astype(F32).astype(BF16)
        y = y + cols[:, 2 + k:3 + k] * dot(sel, z_all)
    y_out[...] = y.astype(BF16)


def solution(mesh):
    row_spec = P(("dp", "cp", "tp"), None)
    head_spec = P(None, "tp", None)
    expert_spec = P(("cp", "tp"), None, None)
    any_spec = pl.BlockSpec(memory_space=pl.ANY)
    vm = pl.BlockSpec(memory_space=pltpu.VMEM)
    DMA = pltpu.SemaphoreType.DMA

    def device_step(x, w_q, w_k, w_v, w_o, ids, gates, w_gate, w_up, w_down):
        tok, hid = x.shape
        nr = tok // QT
        hd = w_q.shape[1] * w_q.shape[2]
        kd = w_k.shape[1] * w_k.shape[2]
        wq_t = w_q.transpose(1, 2, 0).reshape(hd, hid)
        wk_t = w_k.transpose(1, 2, 0).reshape(kd, hid)
        wv_t = w_v.transpose(1, 2, 0).reshape(kd, hid)
        wo = w_o.reshape(hd, hid)
        seq = 8 * tok
        nk = 2 * tok // KC
        npair = w_q.shape[1] // 2
        f = w_gate.shape[2]

        h, wg_r, wu_r, wd_r = pl.pallas_call(
            attn_kernel,
            out_shape=[
                jax.ShapeDtypeStruct((tok, hid), BF16),
                jax.ShapeDtypeStruct((hid, f), BF16),
                jax.ShapeDtypeStruct((hid, f), BF16),
                jax.ShapeDtypeStruct((f, hid), BF16),
            ],
            in_specs=[any_spec] * 8,
            out_specs=[vm, any_spec, any_spec, any_spec],
            scratch_shapes=[
                pltpu.VMEM((2, 2 * tok, hid), BF16),
                pltpu.VMEM((hd, hid), BF16),
                pltpu.VMEM((2 * kd, hid), BF16),
                pltpu.VMEM((4, hd, hid), BF16),
                pltpu.VMEM((2, nk, 2 * kd, KC), BF16),
                pltpu.VMEM((2, nk, 2 * kd, KC), BF16),
                pltpu.VMEM((2, seq, 128), BF16),
                pltpu.VMEM((kd, seq), BF16),
                pltpu.VMEM((4 * nr, npair, 128, 2 * QT), BF16),
                pltpu.VMEM((4 * nr, QT, hd), BF16),
                pltpu.VMEM((tok, 4 * hd), BF16),
                pltpu.VMEM((4 * nr, npair, 1, 2 * QT), F32),
                pltpu.VMEM((4 * nr, npair, 8, 2 * QT), F32),
                pltpu.VMEM((4 * nr, npair, 32, 2 * QT), F32),
                pltpu.VMEM((npair, KC, 2 * QT), F32),
                pltpu.VMEM((npair, 8, 2 * QT), F32),
                DMA((5,)), DMA((nk,)), DMA((nk,)), DMA, DMA, DMA((nk,)), DMA((nk,)),
                DMA((2, nk)), DMA((2, nk)), DMA((9,)), DMA((9,)), DMA((3,)), DMA((3,)),
                DMA((4 * nr,)), DMA((4, nr)),
            ],
            compiler_params=pltpu.CompilerParams(collective_id=0, has_side_effects=True, vmem_limit_bytes=60 * 1024 * 1024),
            name="attn",
        )(x, wq_t, wk_t, wv_t, wo, w_gate, w_up, w_down)

        cap = tok * 2 // 8
        fw = f // 4
        return pl.pallas_call(
            moe_kernel,
            out_shape=jax.ShapeDtypeStruct((tok, hid), BF16),
            in_specs=[vm, vm, vm] + [any_spec] * 6,
            out_specs=vm,
            scratch_shapes=[
                pltpu.VMEM((8, hid, fw), BF16),
                pltpu.VMEM((8, hid, fw), BF16),
                pltpu.VMEM((8, fw, hid), BF16),
                pltpu.VMEM((8, cap, hid), BF16),
                pltpu.VMEM((8, cap, hid), BF16),
                pltpu.VMEM((8, cap, hid), BF16),
                pltpu.VMEM((8, cap, hid), BF16),
                pltpu.VMEM((2 * cap, hid), F32),
                DMA((3, 8)), DMA((8,)), DMA((8,)), DMA((8,)), DMA((8,)),
            ],
            compiler_params=pltpu.CompilerParams(collective_id=1, has_side_effects=True, vmem_limit_bytes=63 * 1024 * 1024),
            name="moe",
        )(h, ids.T, gates.T, w_gate, w_up, w_down, wg_r, wu_r, wd_r)

    return jax.shard_map(device_step, mesh=mesh, in_specs=(row_spec, head_spec, head_spec, head_spec, P("tp", None, None), row_spec, row_spec, expert_spec, expert_spec, expert_spec), out_specs=row_spec, check_vma=False)
```

time: 167 us -> 155 us (0.928)
  Pallas kernels: 164 us -> 153 us
    pallas_call x1, Pallas kernels: 79.9 us -> 69.3 us  [device_step(): pl.pallas_call(moe_kernel, out_shape=jax.ShapeDtypeStruct((tok, hid), BF1...]
where the time goes in v3:
time: 155 us
  Pallas kernels  153 us (99%)
  local copies, waits for them, and re-layouts  2.36 us (2%)
    pallas_call x1, Pallas kernels, device_step(): pl.pallas_call(attn_kernel, out_shape=[jax.ShapeDtypeStruct((tok, hid), B...  83.4 us
    pallas_call x1, Pallas kernels, device_step(): pl.pallas_call(moe_kernel, out_shape=jax.ShapeDtypeStruct((tok, hid), BF1...  69.3 us

profile of v3, /device:TPU:0, one launch (start us, length us, event | category | flops | bytes accessed | tf_op | source)
XLA Modules:
  0.0 155.1 jit_solution(3537509939063038374)
XLA Ops:
  0.0 83.4 %attn.1 = (bf16[384,1536]{1,0:T(8,128)(2,1)}, bf16[1536,2048]{1,0:T(8,128)(2,1)}, bf16[1536,2048]{1,0:T(8,128)(2,1)}, bf16[2048,1536]{1,0:T(8,128)(2,1)}) custom-call(bf16[384,1536]{1,0:T(8,128)(2,1)} %x.1, bf16[384,1536]{1,0:T(8,128)(2,1)} %bitcast.12, bf16[64,1536]{1,0:T(8,128)(2,1)} %bitcast.14, bf16[64,1536]{1,0:T(8,128)(2,1)} %bitcast.15, ...), custom_call_target="tpu_custom_call" | custom-call | tf_op jit(solution)/shard_map/attn/pallas_call | solution.py:529
  83.4 69.3 %moe.1 = bf16[384,1536]{1,0:T(8,128)(2,1)} custom-call(bf16[384,1536]{1,0:T(8,128)(2,1)} %get-tuple-element.9.h, s32[2,384]{1,0:T(2,128)} %bitcast.16, f32[2,384]{1,0:T(2,128)} %bitcast.17, bf16[2,1536,2048]{2,1,0:T(8,128)(2,1)} %wg.3, bf16[2,1536,2048]{2,1,0:T(8,128)(2,1)} %wu.3, bf16[2,2048,1536]{2,1,0:T(8,128)(2,1)} %wd.3, ...), custom_call_target="tpu_custom_call" | custom-call | tf_op jit(solution)/shard_map/moe/pallas_call | solution.py:566
  152.7 2.4 %copy.12 = bf16[384,1536]{1,0:T(8,128)(2,1)} copy(bf16[384,1536]{1,0:T(8,128)(2,1)} %moe.1) | data formatting | bytes 2359296

commit v4 on v3

--- a/solution.py
+++ b/solution.py
@@ -31,7 +31,7 @@
 
 def attn_kernel(x, wq_h, wk_h, wv_h, wo_h, wg, wu, wd,
                 h_out, wg_r, wu_r, wd_r,
-                xh, wq, wkv, wo, kvown, kvrecv, kaug, vt, qaug, osend, orecv, m_s, l_s, acc_s, s_s, mx_s,
+                xh, wq, wkv, wo, kvown, kvrecv, kaug, vt, qaug, osend, orecv, m_s, l_s, acc_s, s_s, mx_s, bias, eye,
                 loc_sem, xf_s, xf_r, xp_s, xp_r, xw_s, xw_r, kv_s, kv_r, wo_s, wo_r, ew_s, ew_r, o_s, o_r):
     c = lax.axis_index("cp")
     t = lax.axis_index("tp")
@@ -120,6 +120,13 @@
 
     zero_pad = jnp.zeros((32, KC), BF16)
 
+    key_i = lax.broadcasted_iota(jnp.int32, (KC, QT), 0)
+    q_i = lax.broadcasted_iota(jnp.int32, (KC, QT), 1)
+    bias[0] = jnp.zeros((KC, QT), BF16)
+    for n in range(2):
+        bias[1 + n] = jnp.where(key_i > q_i + n * QT, -3.38e38, 0.0).astype(BF16)
+    eye[...] = (lax.broadcasted_iota(jnp.int32, (QT, 2 * QT), 0) == lax.rem(lax.broadcasted_iota(jnp.int32, (QT, 2 * QT), 1), QT)).astype(F32).astype(BF16)
+
     def place(kv, ck, k):
         pos = pl.multiple_of((ck * nk + k) * KC, KC)
         for g in range(2):
@@ -174,7 +181,8 @@
     e2 = e1 + 16 + 6 * qq
     njob = 78
     w0 = 8
-    w1 = 60
+    w1 = 52
+    g_ev = (11, 24, 38)
 
     def pick(*pairs):
         out = pairs[-1][1]
@@ -209,16 +217,17 @@
         masked = pick((in1, jnp.where(v1 // 2 == k1, one, zero)), (in2, zero), (in_a, zero), (in_b, jnp.where(ubp // 2 == k, one, zero)), (None, zero))
         last = jnp.where(k == 2, one, zero)
         fin = pick((in1, masked * (1 - xx) * qq), (in2, jnp.where(lax.rem(v2p, 3) == 2, 1 - xx, zero)), (in_c2, last), (in_a, last * xx * jnp.where(ua >= 6, one, zero)), (in_b, masked * pp), (None, last * jnp.where(ucp // 2 == 2, one, zero)))
-        return slot, ch, masked, fin
+        return slot, ch, masked * (1 + lax.rem(slot, 2)), fin
 
     def fold_max(v):
         return jnp.max(v.reshape(KC // 8, 8, 2 * QT), axis=0)
 
-    def score(p, slot, ch):
-        return dot(kaug[p // (npair // 2), pl.ds(pl.multiple_of(ch * KC, KC), KC), :], qaug[slot, p])
+    def score(p, slot, ch, sel):
+        keys = jnp.concatenate([kaug[p // (npair // 2), pl.ds(pl.multiple_of(ch * KC, KC), KC), :], bias[sel]], axis=1)
+        return dot(keys, jnp.concatenate([qaug[slot, p], eye[...]], axis=0))
 
     for p in range(npair):
-        s_first = score(p, 0, lc * nk)
+        s_first = score(p, 0, lc * nk, 1)
         s_s[p] = s_first
         mx_s[p] = fold_max(s_first)
 
@@ -235,73 +244,12 @@
         chip = lax.rem(xx + slot // nt, 2)
         return 2 * chip + u // nr, lax.rem(u, nr)
 
-    def step(i, carry):
-        (slot, ch, masked, fin), following = carry
-        slot_n, ch_n = following[:2]
-        k_ev = pick((i < e1 - 1, 0), (i < e2 - 1, 1), (None, 2))
-        e_ev = pick((i < e1 - 1, e0), (i < e2 - 1, e1), (None, e2))
-
-        @pl.when(i == 2 * nt - 1)
-        def _():
-            def take(k, cc):
-                kvcopy(0, k).wait_recv()
-                place(kvrecv[0, k], ln, k)
-                return cc
-            lax.fori_loop(0, nk, take, 0)
-
-        @pl.when(i == e_ev - 1)
-        def _():
-            xfar(k_ev).wait_recv()
-            xfwd(k_ev).start()
-            xfwd_in(k_ev).wait_recv()
-            project(1, k_ev)
-
-        @pl.when(i == w1)
-        def _():
-            locs[4].wait()
-            for n in range(2):
-                wofar(n).wait_recv()
-                woy(n).start()
-                wofwd(n).start()
-
-        k_r = pick((i < e1, 0), (i < e2, 1), (None, 2))
-        e_r = pick((i < e1, e0), (i < e2, e1), (None, e2))
-
-        @pl.when(i == e_r + 5)
-        def _():
-            kvcopy(1, k_r).wait_recv()
-            place(kvrecv[1, k_r], rn, k_r)
-
-        wi = i - w0
-
-        @pl.when(jnp.logical_and(wi >= 0, wi < 64))
-        def _():
-            wcopy(2, wi, wd.shape[1] // 64).start()
-
-            @pl.when(lax.rem(wi, 2) == 0)
-            def _():
-                wcopy(0, wi // 2, wg.shape[1] // 32).start()
-
-            @pl.when(lax.rem(wi, 2) == 1)
-            def _():
-                wcopy(1, wi // 2, wu.shape[1] // 32).start()
-
-        @pl.when(masked == 1)
-        def _():
-            qpos = ((lc + (slot // nt) * (rc - lc)) * nt + lax.rem(slot, nt)) * QT
-            key_i = lax.broadcasted_iota(jnp.int32, (KC, 2 * QT), 0) + ch * KC
-            q_i = lax.rem(lax.broadcasted_iota(jnp.int32, (KC, 2 * QT), 1), QT) + qpos
-            allowed = key_i <= q_i
-            for p in range(npair):
-                sc = jnp.where(allowed, s_s[p], -jnp.inf)
-                s_s[p] = sc
-                mx_s[p] = fold_max(sc)
-
-        after = job(jnp.minimum(i + 2, njob - 1))
+    def attend(cur, nxt):
+        slot, ch = cur[:2]
         k0 = pl.multiple_of(ch * KC, KC)
         for p in range(npair):
             g = p // (npair // 2)
-            s_next = score(p, slot_n, ch_n)
+            s_next = score(p, *nxt[:3])
             sc = s_s[p]
             m_old = m_s[slot, p]
             m_new = jnp.maximum(m_old, jnp.max(mx_s[p], axis=0, keepdims=True))
@@ -314,26 +262,88 @@
             s_s[p] = s_next
             mx_s[p] = fold_max(s_next)
 
-        @pl.when(fin == 1)
-        def _():
-            pieces = []
-            for p in range(npair):
-                o = acc_s[slot, p] / jnp.sum(l_s[slot, p], axis=0, keepdims=True)
-                pieces += [o[:, :QT], o[:, QT:]]
-            tile_o = jnp.concatenate(pieces, axis=0).T.astype(BF16)
-            b, r = where_of(slot)
-
-            @pl.when(b != t)
+    def finish(slot):
+        pieces = []
+        for p in range(npair):
+            o = acc_s[slot, p] / jnp.sum(l_s[slot, p], axis=0, keepdims=True)
+            pieces += [o[:, :QT], o[:, QT:]]
+        osend[slot] = jnp.concatenate(pieces, axis=0).T.astype(BF16)
+        b, r = where_of(slot)
+
+        @pl.when(b != t)
+        def _():
+            ocopy(slot, b, r).start()
+
+        @pl.when(b == t)
+        def _():
+            orecv[pl.ds(pl.multiple_of(r * QT, QT), QT), pl.ds(pl.multiple_of(t * tok, QT), tok)] = osend[slot]
+
+    g_step = [g // 2 for g in g_ev]
+    r_step = [(e + 5) // 2 for e in (e0, e1, e2)]
+
+    def any_of(m, steps):
+        out = m == steps[0]
+        for v in steps[1:]:
+            out = jnp.logical_or(out, m == v)
+        return out
+
+    def step(m, carry):
+        first, second = carry
+        i = 2 * m
+
+        @pl.when(any_of(m, g_step + r_step + [w1 // 2]))
+        def _():
+            @pl.when(m == nt - 1)
             def _():
-                osend[slot] = tile_o
-                ocopy(slot, b, r).start()
-
-            @pl.when(b == t)
+                def take(k, cc):
+                    kvcopy(0, k).wait_recv()
+                    place(kvrecv[0, k], ln, k)
+                    return cc
+                lax.fori_loop(0, nk, take, 0)
+
+            @pl.when(any_of(m, g_step))
             def _():
-                orecv[pl.ds(pl.multiple_of(r * QT, QT), QT), pl.ds(pl.multiple_of(t * tok, QT), tok)] = tile_o
-        return following, after
-
-    lax.fori_loop(0, njob, step, (job(jnp.int32(0)), job(jnp.int32(1))))
+                k_ev = jnp.where(m <= g_step[0], 0, jnp.where(m <= g_step[1], 1, 2))
+                xfar(k_ev).wait_recv()
+                xfwd(k_ev).start()
+                xfwd_in(k_ev).wait_recv()
+                project(1, k_ev)
+
+            @pl.when(m == w1 // 2)
+            def _():
+                locs[4].wait()
+                for n in range(2):
+                    wofar(n).wait_recv()
+                    woy(n).start()
+                    wofwd(n).start()
+
+            @pl.when(any_of(m, r_step))
+            def _():
+                k_r = jnp.where(m <= r_step[0], 0, jnp.where(m <= r_step[1], 1, 2))
+                kvcopy(1, k_r).wait_recv()
+                place(kvrecv[1, k_r], rn, k_r)
+
+        wi = m - w0 // 2
+
+        @pl.when(jnp.logical_and(wi >= 0, wi < 32))
+        def _():
+            wcopy(0, wi, wg.shape[1] // 32).start()
+            wcopy(1, wi, wu.shape[1] // 32).start()
+            wcopy(2, wi, wd.shape[1] // 32).start()
+
+        third = job(jnp.minimum(i + 2, njob - 1))
+        fourth = job(jnp.minimum(i + 3, njob - 1))
+        attend(first, second)
+        attend(second, third)
+
+        def done(n, cc):
+            finish(first[0] + n * (second[0] - first[0]))
+            return cc
+
+        lax.fori_loop(1 - first[3], 1 + second[3], done, 0)
+        return third, fourth
+
+    lax.fori_loop(0, njob // 2, step, (job(jnp.int32(0)), job(jnp.int32(1))))
 
     for n in range(2):
         woy(n).wait_recv()
@@ -553,6 +563,8 @@
                 pltpu.VMEM((4 * nr, npair, 32, 2 * QT), F32),
                 pltpu.VMEM((npair, KC, 2 * QT), F32),
                 pltpu.VMEM((npair, 8, 2 * QT), F32),
+                pltpu.VMEM((3, KC, QT), BF16),
+                pltpu.VMEM((QT, 2 * QT), BF16),
                 DMA((5,)), DMA((nk,)), DMA((nk,)), DMA, DMA, DMA((nk,)), DMA((nk,)),
                 DMA((2, nk)), DMA((2, nk)), DMA((9,)), DMA((9,)), DMA((3,)), DMA((3,)),
                 DMA((4 * nr,)), DMA((4, nr)),

time: 155 us -> 140 us (0.903)
  Pallas kernels: 153 us -> 137 us
    pallas_call x1, Pallas kernels: 83.4 us -> 68 us  [device_step(): pl.pallas_call(attn_kernel, out_shape=[jax.ShapeDtypeStruct((tok, hid), B...]
where the time goes in v4:
time: 140 us
  Pallas kernels  137 us (98%)
  local copies, waits for them, and re-layouts  2.36 us (2%)
    pallas_call x1, Pallas kernels, device_step(): pl.pallas_call(moe_kernel, out_shape=jax.ShapeDtypeStruct((tok, hid), BF1...  69.4 us
    pallas_call x1, Pallas kernels, device_step(): pl.pallas_call(attn_kernel, out_shape=[jax.ShapeDtypeStruct((tok, hid), B...  68 us

profile of v4, /device:TPU:0, one launch (start us, length us, event | category | flops | bytes accessed | tf_op | source)
XLA Modules:
  0.0 139.8 jit_solution(14813434923415300846)
XLA Ops:
  0.0 68.0 %attn.1 = (bf16[384,1536]{1,0:T(8,128)(2,1)}, bf16[1536,2048]{1,0:T(8,128)(2,1)}, bf16[1536,2048]{1,0:T(8,128)(2,1)}, bf16[2048,1536]{1,0:T(8,128)(2,1)}) custom-call(bf16[384,1536]{1,0:T(8,128)(2,1)} %x.1, bf16[384,1536]{1,0:T(8,128)(2,1)} %bitcast.12, bf16[64,1536]{1,0:T(8,128)(2,1)} %bitcast.14, bf16[64,1536]{1,0:T(8,128)(2,1)} %bitcast.15, ...), custom_call_target="tpu_custom_call" | custom-call | tf_op jit(solution)/shard_map/attn/pallas_call | solution.py:539
  68.1 69.4 %moe.1 = bf16[384,1536]{1,0:T(8,128)(2,1)} custom-call(bf16[384,1536]{1,0:T(8,128)(2,1)} %get-tuple-element.9.h, s32[2,384]{1,0:T(2,128)} %bitcast.16, f32[2,384]{1,0:T(2,128)} %bitcast.17, bf16[2,1536,2048]{2,1,0:T(8,128)(2,1)} %wg.3, bf16[2,1536,2048]{2,1,0:T(8,128)(2,1)} %wu.3, bf16[2,2048,1536]{2,1,0:T(8,128)(2,1)} %wd.3, ...), custom_call_target="tpu_custom_call" | custom-call | tf_op jit(solution)/shard_map/moe/pallas_call | solution.py:578
  137.5 2.4 %copy.12 = bf16[384,1536]{1,0:T(8,128)(2,1)} copy(bf16[384,1536]{1,0:T(8,128)(2,1)} %moe.1) | data formatting | bytes 2359296

commit v5 on v4

--- a/solution.py
+++ b/solution.py
@@ -15,6 +15,7 @@
 NT = (((1,), (1,)), ((), ()))
 QT = 128
 KC = 256
+QW = QT + QT
 
 
 def dot(a, b):
@@ -57,10 +58,8 @@
     qq = 1 - pp
 
     bar = pltpu.get_barrier_semaphore()
-    pl.semaphore_signal(bar, inc=1, device_id={"tp": part}, device_id_type=MESH)
-    pl.semaphore_signal(bar, inc=1, device_id={"tp": far}, device_id_type=MESH)
-    pl.semaphore_signal(bar, inc=1, device_id={"tp": farp}, device_id_type=MESH)
-    pl.semaphore_signal(bar, inc=1, device_id={"cp": cn}, device_id_type=MESH)
+    for dev in ({"tp": part}, {"tp": far}, {"tp": farp}, {"cp": cn}):
+        pl.semaphore_signal(bar, device_id=dev, device_id_type=MESH)
 
     own_rows = pl.ds(pl.multiple_of(s * tok, QT), tok)
     locs = [
@@ -112,7 +111,7 @@
         xfar(0).start()
         xfar(1).start()
 
-    qaug[:, :, 96:128, :] = jnp.zeros((qaug.shape[0], npair, 32, 2 * QT), BF16)
+    qaug[:, :, 96:128, :] = jnp.zeros((qaug.shape[0], npair, 32, QW), BF16)
     kaug[:, :, 96:128] = jnp.zeros((2, kaug.shape[1], 32), BF16)
     m_s[...] = jnp.full(m_s.shape, -jnp.inf, F32)
     l_s[...] = jnp.zeros(l_s.shape, F32)
@@ -125,7 +124,7 @@
     bias[0] = jnp.zeros((KC, QT), BF16)
     for n in range(2):
         bias[1 + n] = jnp.where(key_i > q_i + n * QT, -3.38e38, 0.0).astype(BF16)
-    eye[...] = (lax.broadcasted_iota(jnp.int32, (QT, 2 * QT), 0) == lax.rem(lax.broadcasted_iota(jnp.int32, (QT, 2 * QT), 1), QT)).astype(F32).astype(BF16)
+    eye[...] = (lax.broadcasted_iota(jnp.int32, (QT, QW), 0) == lax.rem(lax.broadcasted_iota(jnp.int32, (QT, QW), 1), QT)).astype(F32).astype(BF16)
 
     def place(kv, ck, k):
         pos = pl.multiple_of((ck * nk + k) * KC, KC)
@@ -220,7 +219,7 @@
         return slot, ch, masked * (1 + lax.rem(slot, 2)), fin
 
     def fold_max(v):
-        return jnp.max(v.reshape(KC // 8, 8, 2 * QT), axis=0)
+        return jnp.max(v.reshape(KC // 8, 8, QW), axis=0)
 
     def score(p, slot, ch, sel):
         keys = jnp.concatenate([kaug[p // (npair // 2), pl.ds(pl.multiple_of(ch * KC, KC), KC), :], bias[sel]], axis=1)
@@ -255,7 +254,7 @@
             m_new = jnp.maximum(m_old, jnp.max(mx_s[p], axis=0, keepdims=True))
             alpha = jnp.exp2(m_old - m_new)
             pr = jnp.exp2(sc - m_new)
-            l_s[slot, p] = l_s[slot, p] * alpha + jnp.sum(pr.reshape(KC // 8, 8, 2 * QT), axis=0)
+            l_s[slot, p] = l_s[slot, p] * alpha + jnp.sum(pr.reshape(KC // 8, 8, QW), axis=0)
             pv = dot(vt[g * 32:(g + 1) * 32, pl.ds(k0, KC)], pr.astype(BF16))
             acc_s[slot, p] = acc_s[slot, p] * alpha + pv
             m_s[slot, p] = m_new
@@ -391,7 +390,7 @@
 
 def moe_kernel(h, ids, gates, wg, wu, wd, wg_r, wu_r, wd_r,
                y_out,
-               g_v, u_v, d_v, send, recv, zsend, zret, zacc,
+               g_v, u_v, d_v, send, recv, zsend, zret, zacc, y_acc,
                w_sem, s_s, s_r, z_s, z_r):
     c = lax.axis_index("cp")
     t = lax.axis_index("tp")
@@ -404,14 +403,16 @@
     half = nf // 2
 
     def peer(r):
-        return {"cp": lax.rem(c + (r // 2) % 2, 2), "tp": 2 * lax.rem(xx + r // 4, 2) + lax.rem(s + r % 2, 2)}
-
-    def peer_dyn(r):
-        return {"cp": lax.rem(c + lax.rem(r // 2, 2), 2), "tp": 2 * lax.rem(xx + r // 4, 2) + lax.rem(s + lax.rem(r, 2), 2)}
+        diag = r // 6
+        mid = jnp.logical_and(r >= 2, r < 6)
+        dy = jnp.where(mid, lax.rem(r, 2), diag)
+        dx = jnp.where(mid, 1 - dy, diag)
+        ds = jnp.where(mid, r // 2 - 1, lax.rem(r, 2))
+        return {"cp": lax.rem(c + dy, 2), "tp": 2 * lax.rem(xx + dx, 2) + lax.rem(s + ds, 2)}
 
     bar = pltpu.get_barrier_semaphore()
     for r in range(1, 8):
-        pl.semaphore_signal(bar, inc=1, device_id=peer(r), device_id_type=MESH)
+        pl.semaphore_signal(bar, device_id=peer(jnp.int32(r)), device_id_type=MESH)
 
     def wload(f, own):
         if own:
@@ -427,7 +428,10 @@
             cp_.start()
 
     ids_v = ids[...]
-    rel = lax.rem(ids_v // 2 + xx, 2) * 4 + lax.rem(ids_v // 4 + c, 2) * 2 + lax.rem(ids_v + s, 2)
+    dx = lax.rem(ids_v // 2 + xx, 2)
+    dy = lax.rem(ids_v // 4 + c, 2)
+    ds = lax.rem(ids_v + s, 2)
+    rel = jnp.where(dx == dy, 6 * dx + ds, 2 + 2 * ds + dy)
     ex_i = lax.broadcasted_iota(jnp.int32, (8, tok), 0)
     oh0 = (rel[0:1] == ex_i).astype(F32)
     oh1 = (rel[1:2] == ex_i).astype(F32)
@@ -446,20 +450,19 @@
         return dot(sel, h[...]).astype(BF16)
 
     def scopy(r):
-        return remote(send.at[r], recv.at[r], s_s.at[r], s_r.at[r], **peer_dyn(r))
+        return remote(send.at[r], recv.at[r], s_s.at[r], s_r.at[r], **peer(r))
 
     def zcopy(r):
-        return remote(zsend.at[r], zret.at[r], z_s.at[r], z_r.at[r], **peer_dyn(r))
+        return remote(zsend.at[r], zret.at[r], z_s.at[r], z_r.at[r], **peer(r))
 
     pl.semaphore_wait(bar, 7)
-    for r in (4, 2, 5, 3, 1, 6, 7):
+    for r in (2, 3, 1, 4, 5, 6, 7):
         send[r] = block(r)
-        scopy(r).start()
+        scopy(jnp.int32(r)).start()
     recv[0] = block(0)
 
-    def group(gi, carry):
-        g = lax.rem(gi, 2) * 2 + gi // 2
-        @pl.when(gi > 0)
+    def group(g, carry):
+        @pl.when(g > 0)
         def _():
             scopy(2 * g).wait_recv()
         scopy(2 * g + 1).wait_recv()
@@ -467,12 +470,12 @@
         zacc[...] = jnp.zeros(zacc.shape, F32)
 
         def fstep(f, cc):
-            @pl.when(jnp.logical_and(gi == 0, f < half))
+            @pl.when(jnp.logical_and(g == 0, f < half))
             def _():
                 for cp_ in wload(f, True):
                     cp_.wait()
 
-            @pl.when(jnp.logical_and(gi == 0, f >= half))
+            @pl.when(jnp.logical_and(g == 0, f >= half))
             def _():
                 for cp_ in wload(f, False):
                     cp_.wait()
@@ -486,12 +489,12 @@
         lax.fori_loop(0, nf, fstep, 0)
         z = zacc[...].astype(BF16)
 
-        @pl.when(gi > 0)
+        @pl.when(g > 0)
         def _():
             zsend[2 * g] = z[:cap]
             zcopy(2 * g).start()
 
-        @pl.when(gi == 0)
+        @pl.when(g == 0)
         def _():
             zret[0] = z[:cap]
 
@@ -502,16 +505,32 @@
     lax.fori_loop(0, 4, group, 0)
 
     cols = jnp.concatenate([slot0, slot1, gates[...], jnp.zeros((4, tok), F32)], axis=0).T
-    for r in range(1, 8):
-        scopy(r).wait_send()
-        zcopy(r).wait()
-    slot_i = lax.broadcasted_iota(jnp.int32, (tok, 8 * cap), 1).astype(F32)
-    z_all = zret[...].reshape(8 * cap, hid)
-    y = h[...].astype(F32)
-    for k in range(2):
-        sel = (cols[:, k:k + 1] == slot_i).astype(F32).astype(BF16)
-        y = y + cols[:, 2 + k:3 + k] * dot(sel, z_all)
-    y_out[...] = y.astype(BF16)
+    slot_i = lax.broadcasted_iota(jnp.int32, (tok, 2 * cap), 1).astype(F32)
+
+    def combine(g, y):
+        z = zret[pl.ds(2 * g, 2)].reshape(2 * cap, hid)
+        want = slot_i + (2 * cap * g).astype(F32)
+        for k in range(2):
+            sel = (cols[:, k:k + 1] == want).astype(F32).astype(BF16)
+            y = y + cols[:, 2 + k:3 + k] * dot(sel, z)
+        return y
+
+    def returned(g, cc):
+        @pl.when(g > 0)
+        def _():
+            scopy(2 * g).wait_send()
+            zcopy(2 * g).wait()
+        scopy(2 * g + 1).wait_send()
+        zcopy(2 * g + 1).wait()
+
+        @pl.when(g < 3)
+        def _():
+            y_acc[...] = combine(g, y_acc[...])
+        return cc
+
+    y_acc[...] = h[...].astype(F32)
+    lax.fori_loop(0, 4, returned, 0)
+    y_out[...] = combine(jnp.int32(3), y_acc[...]).astype(BF16)
 
 
 def solution(mesh):
@@ -551,22 +570,21 @@
                 pltpu.VMEM((hd, hid), BF16),
                 pltpu.VMEM((2 * kd, hid), BF16),
                 pltpu.VMEM((4, hd, hid), BF16),
-                pltpu.VMEM((2, nk, 2 * kd, KC), BF16),
-                pltpu.VMEM((2, nk, 2 * kd, KC), BF16),
+                *[pltpu.VMEM((2, nk, 2 * kd, KC), BF16)] * 2,
                 pltpu.VMEM((2, seq, 128), BF16),
                 pltpu.VMEM((kd, seq), BF16),
-                pltpu.VMEM((4 * nr, npair, 128, 2 * QT), BF16),
+                pltpu.VMEM((4 * nr, npair, 128, QW), BF16),
                 pltpu.VMEM((4 * nr, QT, hd), BF16),
                 pltpu.VMEM((tok, 4 * hd), BF16),
-                pltpu.VMEM((4 * nr, npair, 1, 2 * QT), F32),
-                pltpu.VMEM((4 * nr, npair, 8, 2 * QT), F32),
-                pltpu.VMEM((4 * nr, npair, 32, 2 * QT), F32),
-                pltpu.VMEM((npair, KC, 2 * QT), F32),
-                pltpu.VMEM((npair, 8, 2 * QT), F32),
+                pltpu.VMEM((4 * nr, npair, 1, QW), F32),
+                pltpu.VMEM((4 * nr, npair, 8, QW), F32),
+                pltpu.VMEM((4 * nr, npair, 32, QW), F32),
+                pltpu.VMEM((npair, KC, QW), F32),
+                pltpu.VMEM((npair, 8, QW), F32),
                 pltpu.VMEM((3, KC, QT), BF16),
-                pltpu.VMEM((QT, 2 * QT), BF16),
-                DMA((5,)), DMA((nk,)), DMA((nk,)), DMA, DMA, DMA((nk,)), DMA((nk,)),
-                DMA((2, nk)), DMA((2, nk)), DMA((9,)), DMA((9,)), DMA((3,)), DMA((3,)),
+                pltpu.VMEM((QT, QW), BF16),
+                DMA((5,)), *[DMA((nk,))] * 2, DMA, DMA, *[DMA((nk,))] * 2,
+                *[DMA((2, nk))] * 2, *[DMA((9,))] * 2, *[DMA((3,))] * 2,
                 DMA((4 * nr,)), DMA((4, nr)),
             ],
             compiler_params=pltpu.CompilerParams(collective_id=0, has_side_effects=True, vmem_limit_bytes=60 * 1024 * 1024),
@@ -574,22 +592,22 @@
         )(x, wq_t, wk_t, wv_t, wo, w_gate, w_up, w_down)
 
         cap = tok * 2 // 8
-        fw = f // 4
+        fw = f // 2
+        nf = 2 * f // fw
+        n_dev = 8
         return pl.pallas_call(
             moe_kernel,
             out_shape=jax.ShapeDtypeStruct((tok, hid), BF16),
             in_specs=[vm, vm, vm] + [any_spec] * 6,
             out_specs=vm,
             scratch_shapes=[
-                pltpu.VMEM((8, hid, fw), BF16),
-                pltpu.VMEM((8, hid, fw), BF16),
-                pltpu.VMEM((8, fw, hid), BF16),
-                pltpu.VMEM((8, cap, hid), BF16),
-                pltpu.VMEM((8, cap, hid), BF16),
-                pltpu.VMEM((8, cap, hid), BF16),
-                pltpu.VMEM((8, cap, hid), BF16),
+                pltpu.VMEM((nf, hid, fw), BF16),
+                pltpu.VMEM((nf, hid, fw), BF16),
+                pltpu.VMEM((nf, fw, hid), BF16),
+                *[pltpu.VMEM((n_dev, cap, hid), BF16)] * 4,
                 pltpu.VMEM((2 * cap, hid), F32),
-                DMA((3, 8)), DMA((8,)), DMA((8,)), DMA((8,)), DMA((8,)),
+                pltpu.VMEM((tok, hid), F32),
+                DMA((3, nf)), *[DMA((n_dev,))] * 4,
             ],
             compiler_params=pltpu.CompilerParams(collective_id=1, has_side_effects=True, vmem_limit_bytes=63 * 1024 * 1024),
             name="moe",

time: 140 us -> 130 us (0.929)
  Pallas kernels: 137 us -> 128 us
    pallas_call x1, Pallas kernels: 69.4 us -> 59.5 us  [device_step(): pl.pallas_call(moe_kernel, out_shape=jax.ShapeDtypeStruct((tok, hid), BF1...]
where the time goes in v5:
time: 130 us
  Pallas kernels  128 us (98%)
  local copies, waits for them, and re-layouts  2.36 us (2%)
    pallas_call x1, Pallas kernels, device_step(): pl.pallas_call(attn_kernel, out_shape=[jax.ShapeDtypeStruct((tok, hid), B...  68 us
    pallas_call x1, Pallas kernels, device_step(): pl.pallas_call(moe_kernel, out_shape=jax.ShapeDtypeStruct((tok, hid), BF1...  59.5 us

profile of v5, /device:TPU:0, one launch (start us, length us, event | category | flops | bytes accessed | tf_op | source)
XLA Modules:
  0.0 130.0 jit_solution(12607311287687081227)
XLA Ops:
  0.0 68.0 %attn.1 = (bf16[384,1536]{1,0:T(8,128)(2,1)}, bf16[1536,2048]{1,0:T(8,128)(2,1)}, bf16[1536,2048]{1,0:T(8,128)(2,1)}, bf16[2048,1536]{1,0:T(8,128)(2,1)}) custom-call(bf16[384,1536]{1,0:T(8,128)(2,1)} %x.1, bf16[384,1536]{1,0:T(8,128)(2,1)} %bitcast.12, bf16[64,1536]{1,0:T(8,128)(2,1)} %bitcast.14, bf16[64,1536]{1,0:T(8,128)(2,1)} %bitcast.15, ...), custom_call_target="tpu_custom_call" | custom-call | tf_op jit(solution)/shard_map/attn/pallas_call | solution.py:558
  68.1 59.5 %moe.1 = bf16[384,1536]{1,0:T(8,128)(2,1)} custom-call(bf16[384,1536]{1,0:T(8,128)(2,1)} %get-tuple-element.9.h, s32[2,384]{1,0:T(2,128)} %bitcast.16, f32[2,384]{1,0:T(2,128)} %bitcast.17, bf16[2,1536,2048]{2,1,0:T(8,128)(2,1)} %wg.3, bf16[2,1536,2048]{2,1,0:T(8,128)(2,1)} %wu.3, bf16[2,2048,1536]{2,1,0:T(8,128)(2,1)} %wd.3, ...), custom_call_target="tpu_custom_call" | custom-call | tf_op jit(solution)/shard_map/moe/pallas_call | solution.py:598
  127.6 2.4 %copy.12 = bf16[384,1536]{1,0:T(8,128)(2,1)} copy(bf16[384,1536]{1,0:T(8,128)(2,1)} %moe.1) | data formatting | bytes 2359296

commit v6 on v5

--- a/solution.py
+++ b/solution.py
@@ -32,7 +32,7 @@
 
 def attn_kernel(x, wq_h, wk_h, wv_h, wo_h, wg, wu, wd,
                 h_out, wg_r, wu_r, wd_r,
-                xh, wq, wkv, wo, kvown, kvrecv, kaug, vt, qaug, osend, orecv, m_s, l_s, acc_s, s_s, mx_s, bias, eye,
+                xh, wq, wkv, wo, kvown, kvrecv, kaug, vt, qaug, osend, orecv, m_s, l_s, acc_s, s_s, mx_s, bias, eye, h_s,
                 loc_sem, xf_s, xf_r, xp_s, xp_r, xw_s, xw_r, kv_s, kv_r, wo_s, wo_r, ew_s, ew_r, o_s, o_r):
     c = lax.axis_index("cp")
     t = lax.axis_index("tp")
@@ -180,7 +180,7 @@
     e2 = e1 + 16 + 6 * qq
     njob = 78
     w0 = 8
-    w1 = 52
+    w_step = [25, 31]
     g_ev = (11, 24, 38)
 
     def pick(*pairs):
@@ -192,30 +192,41 @@
     def job(i):
         k1 = pick((i < 2, 0), (i < 6, 1), (None, 2))
         v1 = i - k1 * (k1 + 1)
-        v2 = i - 2 * nt
+        v2 = jnp.maximum(i - 2 * nt, 0)
         k = pick((i < e1, 0), (i < e2, 1), (None, 2))
-        u = i - pick((i < e1, e0), (i < e2, e1), (None, e2))
-        nc2 = qq * 2 * k
-        ua = jnp.where(u < 6, u, u - nc2)
-        ub = u - 12 - nc2
-        uc = ub - 2 * (k + 1)
+        u = jnp.maximum(i - pick((i < e1, e0), (i < e2, e1), (None, e2)), 0)
+        k_1 = k + 1
+        pre = jnp.where(k == 2, 4 * qq, 0)
+        ub = jnp.maximum(u - pre, 0)
+        ua = u - pre - 2 * k_1
+        w = ua - nt
+        v = w - qq * 2 * k + pre
+        len1 = qq * k_1 * (1 + xx)
+        v3 = v - len1
         in1 = i < 2 * nt
         in2 = i < e0
-        in_c2 = jnp.logical_and(u >= 6, u < 6 + nc2)
-        in_a = u < 12 + nc2
-        in_b = ub < 2 * (k + 1)
+        in_pre = u < pre
+        in_b = ua < 0
+        in_a2 = jnp.logical_and(v3 >= 0, v3 < nt)
+        in_a = jnp.logical_or(w < 0, in_a2)
+        in_c2 = v < 0
+        na = jnp.maximum(jnp.where(w < 0, ua, v3), 0)
+        half = jnp.where(in_a2, 1, 0)
+        uc = jnp.maximum(jnp.where(v3 < 0, v, v - nt), 0)
+        tc = pick((k == 0, uc), (k == 1, uc // 2), (None, uc // 3))
+        far_tile = nt + 2 * k
         first = xx == 0
-        slot_a = jnp.where(first, nt + 2 * k + ua // 6, lax.rem(jnp.maximum(ua, 0), 6))
-        ch_a = jnp.where(first, jnp.where(lax.rem(jnp.maximum(ua, 0), 6) < 3, lc, ln) * nk + lax.rem(jnp.maximum(ua, 0), 3), jnp.where(ua < 6, rc, rn) * nk + k)
-        ubp = jnp.maximum(ub, 0)
-        ucp = jnp.maximum(uc, 0)
-        v2p = jnp.maximum(v2, 0)
-        slot = pick((in1, 2 * k1 + lax.rem(jnp.maximum(v1, 0), 2)), (in2, v2p // 3), (in_c2, nt + u - 6), (in_a, slot_a), (in_b, nt + 2 * k + lax.rem(ubp, 2)), (None, nt + 2 * k + lax.rem(ucp, 2)))
-        ch = pick((in1, lc * nk + v1 // 2), (in2, ln * nk + lax.rem(v2p, 3)), (in_c2, rn * nk + k), (in_a, ch_a), (in_b, rc * nk + ubp // 2), (None, rn * nk + ucp // 2))
-        one, zero = jnp.int32(1), jnp.int32(0)
-        masked = pick((in1, jnp.where(v1 // 2 == k1, one, zero)), (in2, zero), (in_a, zero), (in_b, jnp.where(ubp // 2 == k, one, zero)), (None, zero))
-        last = jnp.where(k == 2, one, zero)
-        fin = pick((in1, masked * (1 - xx) * qq), (in2, jnp.where(lax.rem(v2p, 3) == 2, 1 - xx, zero)), (in_c2, last), (in_a, last * xx * jnp.where(ua >= 6, one, zero)), (in_b, masked * pp), (None, last * jnp.where(ucp // 2 == 2, one, zero)))
+        slot_a = jnp.where(first, far_tile + half, na)
+        ch_a = jnp.where(first, jnp.where(na < nk, lc, ln) * nk + lax.rem(na, nk), (rc + half * (rn - rc)) * nk + k)
+        slot = pick((in1, 2 * k1 + lax.rem(v1, 2)), (in2, v2 // nk), (in_pre, nt + u), (in_b, far_tile + lax.rem(ub, 2)), (in_a, slot_a), (in_c2, nt + w), (None, far_tile + tc))
+        ch = pick((in1, lc * nk + v1 // 2), (in2, ln * nk + lax.rem(v2, nk)), (in_pre, rn * nk + k), (in_b, rc * nk + ub // 2), (in_a, ch_a), (in_c2, rn * nk + k), (None, rn * nk + uc - tc * k_1))
+
+        def flag(cond):
+            return jnp.where(cond, 1, 0)
+
+        masked = pick((in1, flag(v1 // 2 == k1)), (in2, 0), (in_pre, 0), (in_b, flag(ub // 2 == k)), (None, 0))
+        last = flag(k == 2)
+        fin = pick((in1, masked * (1 - xx) * qq), (in2, flag(lax.rem(v2, nk) == nk - 1) * (1 - xx)), (in_pre, last), (in_b, masked * pp * xx), (in_a, jnp.where(first, pp * flag(na == nt - 1), last * half)), (in_c2, last), (None, last * flag(uc - tc * k_1 == k)))
         return slot, ch, masked * (1 + lax.rem(slot, 2)), fin
 
     def fold_max(v):
@@ -278,7 +289,7 @@
             orecv[pl.ds(pl.multiple_of(r * QT, QT), QT), pl.ds(pl.multiple_of(t * tok, QT), tok)] = osend[slot]
 
     g_step = [g // 2 for g in g_ev]
-    r_step = [(e + 5) // 2 for e in (e0, e1, e2)]
+    r_step = [(e0 + 7) // 2, (e1 + 9) // 2, (e2 - 1) // 2]
 
     def any_of(m, steps):
         out = m == steps[0]
@@ -290,7 +301,7 @@
         first, second = carry
         i = 2 * m
 
-        @pl.when(any_of(m, g_step + r_step + [w1 // 2]))
+        @pl.when(any_of(m, g_step + r_step + w_step))
         def _():
             @pl.when(m == nt - 1)
             def _():
@@ -308,10 +319,9 @@
                 xfwd_in(k_ev).wait_recv()
                 project(1, k_ev)
 
-            @pl.when(m == w1 // 2)
-            def _():
-                locs[4].wait()
-                for n in range(2):
+            for n in range(2):
+                @pl.when(m == w_step[n])
+                def _(n=n):
                     wofar(n).wait_recv()
                     woy(n).start()
                     wofwd(n).start()
@@ -348,32 +358,54 @@
         woy(n).wait_recv()
         wofwdy(n).start()
 
-    def odone(slot, carry):
-        b, r = where_of(slot)
-
-        @pl.when(b != t)
-        def _():
-            ocopy(slot, b, r).wait_send()
+    def o_from(b):
+        def take(r, cc):
             remote(osend.at[0], orecv.at[pl.ds(pl.multiple_of(r * QT, QT), QT), pl.ds(pl.multiple_of(b * tok, QT), tok)], o_s.at[0], o_r.at[b, r], tp=b).wait_recv()
+            return cc
+        lax.fori_loop(0, nr, take, 0)
+
+    nw = hid // 4
+    near, away = 2 * xx, 2 - 2 * xx
+
+    def part_out(chip, n):
+        sl = pl.ds(pl.multiple_of(n * nw, QT), nw)
+        o = orecv[:, pl.ds(pl.multiple_of(chip * tok, QT), 2 * tok)]
+        return sl, dot(o, wo[pl.ds(chip, 2), :, sl].reshape(2 * tok, nw))
+
+    def near_out(n, carry):
+        sl, ow = part_out(near, n)
+        h_s[:, sl] = xh[0, own_rows, sl].astype(F32) + ow
         return carry
 
-    lax.fori_loop(0, 2 * nt, odone, 0)
+    def far_out(n, carry):
+        sl, ow = part_out(away, n)
+        h_out[:, sl] = (h_s[:, sl] + ow).astype(BF16)
+        return carry
+
+    o_from(part)
+    locs[4].wait()
     wopart.wait()
+    lax.fori_loop(0, 4, near_out, 0)
+    o_from(far)
+    o_from(farp)
+    for n in range(2):
+        wofwd(n).wait()
+        wofwdy(n).wait()
+    lax.fori_loop(0, 4, far_out, 0)
+
     for n in range(2):
         wofar(n).wait_send()
         woy(n).wait_send()
-        wofwd(n).wait()
-        wofwdy(n).wait()
-
-    nw = hid // 4
-
-    def proj_out(n, carry):
-        sl = pl.ds(pl.multiple_of(n * nw, QT), nw)
-        ow = dot(orecv[...], wo[:, :, sl].reshape(hid, nw))
-        h_out[:, sl] = (xh[0, own_rows, sl].astype(F32) + ow).astype(BF16)
+
+    def odone(slot, carry):
+        b, r = where_of(slot)
+
+        @pl.when(b != t)
+        def _():
+            ocopy(slot, b, r).wait_send()
         return carry
 
-    lax.fori_loop(0, 4, proj_out, 0)
+    lax.fori_loop(0, 2 * nt, odone, 0)
 
     def drain(k, carry):
         kvcopy(0, k).wait_send()
@@ -583,6 +615,7 @@
                 pltpu.VMEM((npair, 8, QW), F32),
                 pltpu.VMEM((3, KC, QT), BF16),
                 pltpu.VMEM((QT, QW), BF16),
+                pltpu.VMEM((tok, hid), F32),
                 DMA((5,)), *[DMA((nk,))] * 2, DMA, DMA, *[DMA((nk,))] * 2,
                 *[DMA((2, nk))] * 2, *[DMA((9,))] * 2, *[DMA((3,))] * 2,
                 DMA((4 * nr,)), DMA((4, nr)),

time: 130 us -> 130 us (level)
    pallas_call x1, Pallas kernels: 68 us -> 65.7 us  [device_step(): pl.pallas_call(attn_kernel, out_shape=[jax.ShapeDtypeStruct((tok, hid), B...]
    pallas_call x1, Pallas kernels: 59.5 us -> 61.6 us  [device_step(): pl.pallas_call(moe_kernel, out_shape=jax.ShapeDtypeStruct((tok, hid), BF1...]
where the time goes in v6:
time: 130 us
  Pallas kernels  127 us (98%)
  local copies, waits for them, and re-layouts  2.36 us (2%)
    pallas_call x1, Pallas kernels, device_step(): pl.pallas_call(attn_kernel, out_shape=[jax.ShapeDtypeStruct((tok, hid), B...  65.7 us
    pallas_call x1, Pallas kernels, device_step(): pl.pallas_call(moe_kernel, out_shape=jax.ShapeDtypeStruct((tok, hid), BF1...  61.6 us

profile of v6, /device:TPU:0, one launch (start us, length us, event | category | flops | bytes accessed | tf_op | source)
XLA Modules:
  0.0 129.7 jit_solution(16995664689205485834)
XLA Ops:
  0.0 65.7 %attn.1 = (bf16[384,1536]{1,0:T(8,128)(2,1)}, bf16[1536,2048]{1,0:T(8,128)(2,1)}, bf16[1536,2048]{1,0:T(8,128)(2,1)}, bf16[2048,1536]{1,0:T(8,128)(2,1)}) custom-call(bf16[384,1536]{1,0:T(8,128)(2,1)} %x.1, bf16[384,1536]{1,0:T(8,128)(2,1)} %bitcast.12, bf16[64,1536]{1,0:T(8,128)(2,1)} %bitcast.14, bf16[64,1536]{1,0:T(8,128)(2,1)} %bitcast.15, ...), custom_call_target="tpu_custom_call" | custom-call | tf_op jit(solution)/shard_map/attn/pallas_call | solution.py:590
  65.7 61.6 %moe.1 = bf16[384,1536]{1,0:T(8,128)(2,1)} custom-call(bf16[384,1536]{1,0:T(8,128)(2,1)} %get-tuple-element.9.h, s32[2,384]{1,0:T(2,128)} %bitcast.16, f32[2,384]{1,0:T(2,128)} %bitcast.17, bf16[2,1536,2048]{2,1,0:T(8,128)(2,1)} %wg.3, bf16[2,1536,2048]{2,1,0:T(8,128)(2,1)} %wu.3, bf16[2,2048,1536]{2,1,0:T(8,128)(2,1)} %wd.3, ...), custom_call_target="tpu_custom_call" | custom-call | tf_op jit(solution)/shard_map/moe/pallas_call | solution.py:631
  127.4 2.4 %copy.12 = bf16[384,1536]{1,0:T(8,128)(2,1)} copy(bf16[384,1536]{1,0:T(8,128)(2,1)} %moe.1) | data formatting | bytes 2359296

commit v7 on v6

--- a/solution.py
+++ b/solution.py
@@ -32,7 +32,7 @@
 
 def attn_kernel(x, wq_h, wk_h, wv_h, wo_h, wg, wu, wd,
                 h_out, wg_r, wu_r, wd_r,
-                xh, wq, wkv, wo, kvown, kvrecv, kaug, vt, qaug, osend, orecv, m_s, l_s, acc_s, s_s, mx_s, bias, eye, h_s,
+                xh, wq, wkv, wo, kvown, kvrecv, kaug, vt, qaug, osend, orecv, m_s, l_s, acc_s, s_s, mx_s, h_s,
                 loc_sem, xf_s, xf_r, xp_s, xp_r, xw_s, xw_r, kv_s, kv_r, wo_s, wo_r, ew_s, ew_r, o_s, o_r):
     c = lax.axis_index("cp")
     t = lax.axis_index("tp")
@@ -119,13 +119,6 @@
 
     zero_pad = jnp.zeros((32, KC), BF16)
 
-    key_i = lax.broadcasted_iota(jnp.int32, (KC, QT), 0)
-    q_i = lax.broadcasted_iota(jnp.int32, (KC, QT), 1)
-    bias[0] = jnp.zeros((KC, QT), BF16)
-    for n in range(2):
-        bias[1 + n] = jnp.where(key_i > q_i + n * QT, -3.38e38, 0.0).astype(BF16)
-    eye[...] = (lax.broadcasted_iota(jnp.int32, (QT, QW), 0) == lax.rem(lax.broadcasted_iota(jnp.int32, (QT, QW), 1), QT)).astype(F32).astype(BF16)
-
     def place(kv, ck, k):
         pos = pl.multiple_of((ck * nk + k) * KC, KC)
         for g in range(2):
@@ -190,22 +183,25 @@
         return out
 
     def job(i):
-        k1 = pick((i < 2, 0), (i < 6, 1), (None, 2))
-        v1 = i - k1 * (k1 + 1)
+        n1 = i // 2
+        odd = lax.rem(i, 2) == 1
+        late = n1 >= 4
         v2 = jnp.maximum(i - 2 * nt, 0)
         k = pick((i < e1, 0), (i < e2, 1), (None, 2))
         u = jnp.maximum(i - pick((i < e1, e0), (i < e2, e1), (None, e2)), 0)
         k_1 = k + 1
         pre = jnp.where(k == 2, 4 * qq, 0)
-        ub = jnp.maximum(u - pre, 0)
-        ua = u - pre - 2 * k_1
+        um = u - pre
+        ub = jnp.maximum(jnp.where(um < 4, um // 2, um - 2), 0)
+        ua = ub - 2 * k
         w = ua - nt
         v = w - qq * 2 * k + pre
         len1 = qq * k_1 * (1 + xx)
         v3 = v - len1
         in1 = i < 2 * nt
         in2 = i < e0
-        in_pre = u < pre
+        in_pre = um < 0
+        in_m = jnp.logical_or(um == 0, um == 2)
         in_b = ua < 0
         in_a2 = jnp.logical_and(v3 >= 0, v3 < nt)
         in_a = jnp.logical_or(w < 0, in_a2)
@@ -216,28 +212,28 @@
         tc = pick((k == 0, uc), (k == 1, uc // 2), (None, uc // 3))
         far_tile = nt + 2 * k
         first = xx == 0
+
+        def flag(cond):
+            return jnp.where(cond, 1, 0)
+
         slot_a = jnp.where(first, far_tile + half, na)
         ch_a = jnp.where(first, jnp.where(na < nk, lc, ln) * nk + lax.rem(na, nk), (rc + half * (rn - rc)) * nk + k)
-        slot = pick((in1, 2 * k1 + lax.rem(v1, 2)), (in2, v2 // nk), (in_pre, nt + u), (in_b, far_tile + lax.rem(ub, 2)), (in_a, slot_a), (in_c2, nt + w), (None, far_tile + tc))
-        ch = pick((in1, lc * nk + v1 // 2), (in2, ln * nk + lax.rem(v2, nk)), (in_pre, rn * nk + k), (in_b, rc * nk + ub // 2), (in_a, ch_a), (in_c2, rn * nk + k), (None, rn * nk + uc - tc * k_1))
-
-        def flag(cond):
-            return jnp.where(cond, 1, 0)
-
-        masked = pick((in1, flag(v1 // 2 == k1)), (in2, 0), (in_pre, 0), (in_b, flag(ub // 2 == k)), (None, 0))
+        slot_1 = jnp.where(odd, n1 + jnp.where(late, 0, 2), n1)
+        slot = pick((in1, slot_1), (in2, v2 // nk), (in_pre, nt + u), (in_m, far_tile + um // 2), (in_b, far_tile + lax.rem(ub, 2)), (in_a, slot_a), (in_c2, nt + w), (None, far_tile + tc))
+        ch = pick((in1, lc * nk + jnp.where(odd, flag(late), n1 // 2)), (in2, ln * nk + lax.rem(v2, nk)), (in_pre, rn * nk + k), (in_m, rc * nk + k), (in_b, rc * nk + ub // 2), (in_a, ch_a), (in_c2, rn * nk + k), (None, rn * nk + uc - tc * k_1))
+        masked = pick((in1, 1 - flag(odd)), (in2, 0), (in_pre, 0), (in_m, 1), (None, 0))
         last = flag(k == 2)
-        fin = pick((in1, masked * (1 - xx) * qq), (in2, flag(lax.rem(v2, nk) == nk - 1) * (1 - xx)), (in_pre, last), (in_b, masked * pp * xx), (in_a, jnp.where(first, pp * flag(na == nt - 1), last * half)), (in_c2, last), (None, last * flag(uc - tc * k_1 == k)))
-        return slot, ch, masked * (1 + lax.rem(slot, 2)), fin
+        fin = pick((in1, flag(odd == late) * (1 - xx) * qq), (in2, flag(lax.rem(v2, nk) == nk - 1) * (1 - xx)), (in_pre, last), (in_m, flag(k == 0) * pp * xx), (in_b, flag(ub // 2 == k - 1) * pp * xx), (in_a, jnp.where(first, pp * flag(na == nt - 1), last * half)), (in_c2, last), (None, last * flag(uc - tc * k_1 == k)))
+        return slot, ch, masked, fin
 
     def fold_max(v):
         return jnp.max(v.reshape(KC // 8, 8, QW), axis=0)
 
-    def score(p, slot, ch, sel):
-        keys = jnp.concatenate([kaug[p // (npair // 2), pl.ds(pl.multiple_of(ch * KC, KC), KC), :], bias[sel]], axis=1)
-        return dot(keys, jnp.concatenate([qaug[slot, p], eye[...]], axis=0))
+    def score(p, slot, ch):
+        return dot(kaug[p // (npair // 2), pl.ds(pl.multiple_of(ch * KC, KC), KC), :], qaug[slot, p])
 
     for p in range(npair):
-        s_first = score(p, 0, lc * nk, 1)
+        s_first = score(p, 0, lc * nk)
         s_s[p] = s_first
         mx_s[p] = fold_max(s_first)
 
@@ -259,7 +255,7 @@
         k0 = pl.multiple_of(ch * KC, KC)
         for p in range(npair):
             g = p // (npair // 2)
-            s_next = score(p, *nxt[:3])
+            s_next = score(p, *nxt[:2])
             sc = s_s[p]
             m_old = m_s[slot, p]
             m_new = jnp.maximum(m_old, jnp.max(mx_s[p], axis=0, keepdims=True))
@@ -339,6 +335,15 @@
             wcopy(0, wi, wg.shape[1] // 32).start()
             wcopy(1, wi, wu.shape[1] // 32).start()
             wcopy(2, wi, wd.shape[1] // 32).start()
+
+        @pl.when(first[2] == 1)
+        def _():
+            key_i = lax.broadcasted_iota(jnp.int32, (KC, QW), 0)
+            q_i = lax.rem(lax.broadcasted_iota(jnp.int32, (KC, QW), 1), QT) + lax.rem(first[0], 2) * QT
+            for p in range(npair):
+                sc = jnp.where(key_i <= q_i, s_s[p], -jnp.inf)
+                s_s[p] = sc
+                mx_s[p] = fold_max(sc)
 
         third = job(jnp.minimum(i + 2, njob - 1))
         fourth = job(jnp.minimum(i + 3, njob - 1))
@@ -488,7 +493,7 @@
         return remote(zsend.at[r], zret.at[r], z_s.at[r], z_r.at[r], **peer(r))
 
     pl.semaphore_wait(bar, 7)
-    for r in (2, 3, 1, 4, 5, 6, 7):
+    for r in (3, 2, 1, 5, 4, 6, 7):
         send[r] = block(r)
         scopy(jnp.int32(r)).start()
     recv[0] = block(0)
@@ -613,8 +618,6 @@
                 pltpu.VMEM((4 * nr, npair, 32, QW), F32),
                 pltpu.VMEM((npair, KC, QW), F32),
                 pltpu.VMEM((npair, 8, QW), F32),
-                pltpu.VMEM((3, KC, QT), BF16),
-                pltpu.VMEM((QT, QW), BF16),
                 pltpu.VMEM((tok, hid), F32),
                 DMA((5,)), *[DMA((nk,))] * 2, DMA, DMA, *[DMA((nk,))] * 2,
                 *[DMA((2, nk))] * 2, *[DMA((9,))] * 2, *[DMA((3,))] * 2,

time: 130 us -> 124 us (0.954)
  Pallas kernels: 127 us -> 121 us
    pallas_call x1, Pallas kernels: 61.6 us -> 58.2 us  [device_step(): pl.pallas_call(moe_kernel, out_shape=jax.ShapeDtypeStruct((tok, hid), BF1...]
    pallas_call x1, Pallas kernels: 65.7 us -> 63.1 us  [device_step(): pl.pallas_call(attn_kernel, out_shape=[jax.ShapeDtypeStruct((tok, hid), B...]
where the time goes in v7:
time: 124 us
  Pallas kernels  121 us (98%)
  local copies, waits for them, and re-layouts  2.36 us (2%)
    pallas_call x1, Pallas kernels, device_step(): pl.pallas_call(attn_kernel, out_shape=[jax.ShapeDtypeStruct((tok, hid), B...  63.1 us
    pallas_call x1, Pallas kernels, device_step(): pl.pallas_call(moe_kernel, out_shape=jax.ShapeDtypeStruct((tok, hid), BF1...  58.2 us

profile of v7, /device:TPU:0, one launch (start us, length us, event | category | flops | bytes accessed | tf_op | source)
XLA Modules:
  0.0 123.7 jit_solution(10197687352647615918)
XLA Ops:
  0.0 63.1 %attn.1 = (bf16[384,1536]{1,0:T(8,128)(2,1)}, bf16[1536,2048]{1,0:T(8,128)(2,1)}, bf16[1536,2048]{1,0:T(8,128)(2,1)}, bf16[2048,1536]{1,0:T(8,128)(2,1)}) custom-call(bf16[384,1536]{1,0:T(8,128)(2,1)} %x.1, bf16[384,1536]{1,0:T(8,128)(2,1)} %bitcast.12, bf16[64,1536]{1,0:T(8,128)(2,1)} %bitcast.14, bf16[64,1536]{1,0:T(8,128)(2,1)} %bitcast.15, ...), custom_call_target="tpu_custom_call" | custom-call | tf_op jit(solution)/shard_map/attn/pallas_call | solution.py:595
  63.1 58.2 %moe.1 = bf16[384,1536]{1,0:T(8,128)(2,1)} custom-call(bf16[384,1536]{1,0:T(8,128)(2,1)} %get-tuple-element.9.h, s32[2,384]{1,0:T(2,128)} %bitcast.16, f32[2,384]{1,0:T(2,128)} %bitcast.17, bf16[2,1536,2048]{2,1,0:T(8,128)(2,1)} %wg.3, bf16[2,1536,2048]{2,1,0:T(8,128)(2,1)} %wu.3, bf16[2,2048,1536]{2,1,0:T(8,128)(2,1)} %wd.3, ...), custom_call_target="tpu_custom_call" | custom-call | tf_op jit(solution)/shard_map/moe/pallas_call | solution.py:634
  121.3 2.4 %copy.12 = bf16[384,1536]{1,0:T(8,128)(2,1)} copy(bf16[384,1536]{1,0:T(8,128)(2,1)} %moe.1) | data formatting | bytes 2359296

commit v8 on v7

--- a/solution.py
+++ b/solution.py
@@ -173,7 +173,7 @@
     e2 = e1 + 16 + 6 * qq
     njob = 78
     w0 = 8
-    w_step = [25, 31]
+    w_step = [24, 29]
     g_ev = (11, 24, 38)
 
     def pick(*pairs):
@@ -369,7 +369,7 @@
             return cc
         lax.fori_loop(0, nr, take, 0)
 
-    nw = hid // 4
+    nw = hid // 3
     near, away = 2 * xx, 2 - 2 * xx
 
     def part_out(chip, n):
@@ -390,13 +390,13 @@
     o_from(part)
     locs[4].wait()
     wopart.wait()
-    lax.fori_loop(0, 4, near_out, 0)
+    lax.fori_loop(0, hid // nw, near_out, 0)
     o_from(far)
     o_from(farp)
     for n in range(2):
         wofwd(n).wait()
         wofwdy(n).wait()
-    lax.fori_loop(0, 4, far_out, 0)
+    lax.fori_loop(0, hid // nw, far_out, 0)
 
     for n in range(2):
         wofar(n).wait_send()

time: 124 us -> 123 us (level)
    pallas_call x1, Pallas kernels: 63.1 us -> 61.2 us  [device_step(): pl.pallas_call(attn_kernel, out_shape=[jax.ShapeDtypeStruct((tok, hid), B...]
where the time goes in v8:
time: 123 us
  Pallas kernels  120 us (98%)
  local copies, waits for them, and re-layouts  2.36 us (2%)
    pallas_call x1, Pallas kernels, device_step(): pl.pallas_call(attn_kernel, out_shape=[jax.ShapeDtypeStruct((tok, hid), B...  61.2 us
    pallas_call x1, Pallas kernels, device_step(): pl.pallas_call(moe_kernel, out_shape=jax.ShapeDtypeStruct((tok, hid), BF1...  59 us

profile of v8, /device:TPU:0, one launch (start us, length us, event | category | flops | bytes accessed | tf_op | source)
XLA Modules:
  0.0 122.6 jit_solution(3327656181658953252)
XLA Ops:
  0.0 61.2 %attn.1 = (bf16[384,1536]{1,0:T(8,128)(2,1)}, bf16[1536,2048]{1,0:T(8,128)(2,1)}, bf16[1536,2048]{1,0:T(8,128)(2,1)}, bf16[2048,1536]{1,0:T(8,128)(2,1)}) custom-call(bf16[384,1536]{1,0:T(8,128)(2,1)} %x.1, bf16[384,1536]{1,0:T(8,128)(2,1)} %bitcast.12, bf16[64,1536]{1,0:T(8,128)(2,1)} %bitcast.14, bf16[64,1536]{1,0:T(8,128)(2,1)} %bitcast.15, ...), custom_call_target="tpu_custom_call" | custom-call | tf_op jit(solution)/shard_map/attn/pallas_call | solution.py:595
  61.2 59.0 %moe.1 = bf16[384,1536]{1,0:T(8,128)(2,1)} custom-call(bf16[384,1536]{1,0:T(8,128)(2,1)} %get-tuple-element.9.h, s32[2,384]{1,0:T(2,128)} %bitcast.16, f32[2,384]{1,0:T(2,128)} %bitcast.17, bf16[2,1536,2048]{2,1,0:T(8,128)(2,1)} %wg.3, bf16[2,1536,2048]{2,1,0:T(8,128)(2,1)} %wu.3, bf16[2,2048,1536]{2,1,0:T(8,128)(2,1)} %wd.3, ...), custom_call_target="tpu_custom_call" | custom-call | tf_op jit(solution)/shard_map/moe/pallas_call | solution.py:634
  120.2 2.4 %copy.12 = bf16[384,1536]{1,0:T(8,128)(2,1)} copy(bf16[384,1536]{1,0:T(8,128)(2,1)} %moe.1) | data formatting | bytes 2359296
